TPU v7x, 16 devices: a 4x2x1 block of a 4x4x8 slice. The times are simulated.
16 devices in a mesh: rep: 2 (over y, z), dp: 8 (over x, core).
Axes of the slice: x: 4, y: 2, z: 1, core: 2. Of those that a mesh axis runs over, the one named last changes fastest.
The devices are a block of a 4x4x8 slice.
Arguments:
- g_w_gate: bfloat16 [16, 2, 1152, 4608], P(('rep', 'dp')), parts along dimension 0
- g_w_up: bfloat16 [16, 2, 1152, 4608], P(('rep', 'dp')), parts along dimension 0
- g_w_down: bfloat16 [16, 2, 4608, 1152], P(('rep', 'dp')), parts along dimension 0
- w_gate: bfloat16 [2, 1152, 4608], replicated
- w_up: bfloat16 [2, 1152, 4608], replicated
- w_down: bfloat16 [2, 4608, 1152], replicated
- m_w_gate: float32 [2, 1152, 4608], P(None, 'dp')
- m_w_up: float32 [2, 1152, 4608], P(None, 'dp')
- m_w_down: float32 [2, 4608, 1152], P(None, 'dp')
- v_w_gate: float32 [2, 1152, 4608], P(None, 'dp')
- v_w_up: float32 [2, 1152, 4608], P(None, 'dp')
- v_w_down: float32 [2, 4608, 1152], P(None, 'dp')
Outputs:
- output 1: bfloat16 [4, 1152, 4608], P('rep'), parts along dimension 0
- output 2: bfloat16 [4, 1152, 4608], P('rep'), parts along dimension 0
- output 3: bfloat16 [4, 4608, 1152], P('rep'), parts along dimension 0
- output 4: float32 [4, 1152, 4608], P('rep', 'dp'), parts along dimension 0
- output 5: float32 [4, 1152, 4608], P('rep', 'dp'), parts along dimension 0
- output 6: float32 [4, 4608, 1152], P('rep', 'dp'), parts along dimension 0
- output 7: float32 [4, 1152, 4608], P('rep', 'dp'), parts along dimension 0
- output 8: float32 [4, 1152, 4608], P('rep', 'dp'), parts along dimension 0
- output 9: float32 [4, 4608, 1152], P('rep', 'dp'), parts along dimension 0
There are 2 independent parts. A program takes and returns all parts, laid end to end along the dimension named above; an argument that names none is the same for every part.
All inputs are finite; a program needn't handle non-finite values.
Results may differ from a plain program's by a relative error of at most 0.022.
Values are sent between devices in bfloat16 or wider.
A program may use at most 768 MiB of HBM per device.

v0:
```python
import functools

import jax
import jax.numpy as jnp
from jax import lax
from jax.experimental import pallas as pl
from jax.experimental.pallas import tpu as pltpu
from jax.sharding import PartitionSpec as P


CORES = 2
PIECES = 4
STRIP = 16
MESH = pl.DeviceIdType.MESH
ORDER = (2, 1, 3, 0)


def reduce_kernel(chips, layers, parts, *refs):
    weights = 3
    terms, old, ms, vs = (refs[i : i + weights] for i in range(0, 4 * weights, weights))
    units = weights * layers
    count = len(parts)
    outs = refs[4 * weights : 5 * weights + 2 * count + 2]
    fresh, other, grads = outs[:count], outs[count : 2 * count], outs[2 * count : 2 * count + weights]
    first = outs[-2:]
    (own, oth, m_in, v_in, w_in, w_out, g_out, far, near, from_far, from_near,
     own_sem, oth_send, oth_recv, old_sem, out_sem, far_send, far_recv, near_send, near_recv,
     other_send, other_recv, first_send, first_recv, free_sem) = refs[5 * weights + 2 * count + 2 :]
    rows, columns = own.shape[-2:]
    chunks = units * 2
    me = lax.axis_index("dp")
    x, k = me // CORES, lax.rem(me, CORES)
    right = {"dp": lax.rem(x + 1, chips) * CORES + k}
    left = {"dp": lax.rem(x + chips - 1, chips) * CORES + k}
    partner = {"dp": x * CORES + 1 - k}

    barrier = pltpu.get_barrier_semaphore()
    for who in (right, left, partner):
        pl.semaphore_signal(barrier, inc=1, device_id=who, device_id_type=MESH)
    pl.semaphore_wait(barrier, 3)

    def piece(ref, lead, block, p):
        if ref.shape[-1] == columns:
            return ref.at[(*lead, pl.ds(pl.multiple_of((block * PIECES + p) * rows, 8), rows))]
        return ref.at[(*lead, pl.ds(pl.multiple_of(block * rows, 8), rows), pl.ds(pl.multiple_of(p * columns, 128), columns))]

    def for_weight(c, body):
        for i in range(weights):
            pl.when(c // (layers * 2) == i)(functools.partial(body, i, lax.rem(c // 2, layers), lax.rem(c, 2)))

    def load(c):
        slot = lax.rem(c, 4)

        def start(i, layer, h):
            for group in ((0,), (1, 2, 3)):
                late = min(group[0], 1)
                for j in group:
                    block = lax.rem(x + ORDER[j], chips) * CORES
                    for q in range(2):
                        pltpu.make_async_remote_copy(
                            src_ref=piece(terms[i], (0, layer), block + 1 - k, h * 2 + q),
                            dst_ref=oth.at[slot, j, q],
                            send_sem=oth_send.at[slot, late],
                            recv_sem=oth_recv.at[slot, late],
                            device_id=partner,
                            device_id_type=MESH,
                        ).start()
                        pltpu.make_async_copy(piece(terms[i], (0, layer), block + k, h * 2 + q), own.at[slot, j, q], own_sem.at[slot, late]).start()

        for_weight(c, start)

    def load_old(c):
        slot = lax.rem(c, 2)

        def start(i, layer, h):
            for q in range(2):
                p = h * 2 + q
                pltpu.make_async_copy(piece(ms[i], (layer,), 0, p), m_in.at[slot, q], old_sem.at[slot, 0]).start()
                pltpu.make_async_copy(piece(vs[i], (layer,), 0, p), v_in.at[slot, q], old_sem.at[slot, 1]).start()
                pltpu.make_async_copy(piece(old[i], (layer,), me, p), w_in.at[slot, q], old_sem.at[slot, 2]).start()

        for_weight(c, start)

    def wait_for(ref, sem):
        pltpu.make_async_copy(ref, ref, sem).wait()

    def wait_terms(slot, late):
        part = pl.ds(late, 3) if late else pl.ds(0, 1)
        wait_for(own.at[slot, part], own_sem.at[slot, late])
        wait_for(oth.at[slot, part], oth_recv.at[slot, late])
        wait_for(oth.at[slot, part], oth_send.at[slot, late])

    def strips(body):
        @pl.loop(0, rows // STRIP)
        def _(r):
            body(pl.ds(pl.multiple_of(r * STRIP, STRIP), STRIP))

    def pair(slot, j, q, at):
        return own[slot, j, q, at].astype(jnp.float32) + oth[slot, j, q, at].astype(jnp.float32)

    def far_copy(c, q):
        return pltpu.make_async_remote_copy(
            src_ref=far.at[lax.rem(c, 2), q],
            dst_ref=from_far.at[c, q],
            send_sem=far_send.at[lax.rem(c, 2), q],
            recv_sem=far_recv.at[c, q],
            device_id=(right, left)[q],
            device_id_type=MESH,
        )

    def near_copy(c, d):
        return pltpu.make_async_remote_copy(
            src_ref=near.at[lax.rem(c, 2), d],
            dst_ref=from_near.at[c, d],
            send_sem=near_send.at[lax.rem(c, 2), d],
            recv_sem=near_recv.at[c, d],
            device_id=(right, left)[d],
            device_id_type=MESH,
        )

    def send_far(c):
        slot = lax.rem(c, 4)
        wait_terms(slot, 0)

        @pl.when(c >= 2)
        def _():
            for q in range(2):
                far_copy(c - 2, q).wait_send()

        def strip(at):
            for q in range(2):
                far[lax.rem(c, 2), q, at] = pair(slot, 0, q, at).astype(far.dtype)

        strips(strip)
        for q in range(2):
            far_copy(c, q).start()

    def send_near(c):
        slot = lax.rem(c, 4)
        wait_terms(slot, 1)

        @pl.when(c >= 2)
        def _():
            for d in range(2):
                near_copy(c - 2, d).wait_send()

        for q in range(2):
            far_copy(c, q).wait_recv()

        def strip(at):
            for d in range(2):
                for q in range(2):
                    total = pair(slot, 1 + d, q, at)
                    if q == d:
                        total += from_far[c, q, at].astype(jnp.float32)
                    near[lax.rem(c, 2), d, q, at] = total.astype(near.dtype)

        strips(strip)
        for d in range(2):
            near_copy(c, d).start()

    def outputs(c, act, act_remote):
        slot = lax.rem(c, 2)

        def go(i, layer, h):
            for q in range(2):
                p = h * 2 + q
                act(pltpu.make_async_copy(g_out.at[slot, q], piece(grads[i], (layer,), 0, p), out_sem.at[slot, q, 0]))
                for u, (weight, start, size) in enumerate(parts):
                    if weight == i:

                        @pl.when((layer >= start) & (layer < start + size))
                        def _():
                            act(pltpu.make_async_copy(w_out.at[slot, q], piece(fresh[u], (layer - start,), 0, p), out_sem.at[slot, q, 1]))
                            act_remote(
                                pltpu.make_async_remote_copy(
                                    src_ref=w_out.at[slot, q],
                                    dst_ref=piece(other[u], (layer - start,), 0, p),
                                    send_sem=other_send.at[slot, q],
                                    recv_sem=other_recv.at[u],
                                    device_id=partner,
                                    device_id_type=MESH,
                                )
                            )

        for_weight(c, go)

    def start_outputs(c):
        outputs(c, lambda copy: copy.start(), lambda copy: copy.start())

    def wait_outputs(c):
        outputs(c, lambda copy: copy.wait(), lambda copy: copy.wait_send())

    def first_copy(d):
        return pltpu.make_async_remote_copy(
            src_ref=fresh[0],
            dst_ref=first[d],
            send_sem=first_send.at[d],
            recv_sem=first_recv.at[d],
            device_id=(right, left)[d],
            device_id_type=MESH,
        )

    def finish(c):
        slot, two = lax.rem(c, 4), lax.rem(c, 2)
        wait_for(m_in.at[two], old_sem.at[two, 0])
        wait_for(v_in.at[two], old_sem.at[two, 1])
        wait_for(w_in.at[two], old_sem.at[two, 2])

        @pl.when(c >= 2)
        def _():
            wait_outputs(c - 2)

        for d in range(2):
            near_copy(c, d).wait_recv()

        def strip(at):
            for q in range(2):
                total = pair(slot, 3, q, at) + from_near[c, 0, q, at].astype(jnp.float32) + from_near[c, 1, q, at].astype(jnp.float32)
                g = total.astype(g_out.dtype)
                g_out[two, q, at] = g
                g = g.astype(jnp.float32)
                w = w_in[two, q, at].astype(jnp.float32)
                m = 0.9 * m_in[two, q, at] + 0.1 * g
                v = 0.95 * v_in[two, q, at] + 0.05 * g * g
                w_out[two, q, at] = (w - 0.02 * (m * lax.rsqrt(v + 1e-8) + 0.1 * w)).astype(w_out.dtype)

        strips(strip)
        start_outputs(c)

        @pl.when(c + 4 < chunks)
        def _():
            pl.semaphore_signal(free_sem, inc=1, device_id=partner, device_id_type=MESH)

    @pl.loop(0, chunks + 3)
    def _(s):
        @pl.when((s >= 1) & (s < chunks + 1))
        def _():
            send_far(s - 1)

        @pl.when(s < chunks)
        def _():
            @pl.when(s >= 4)
            def _():
                pl.semaphore_wait(free_sem, 1)

            load(s)

        @pl.when((s >= 2) & (s < chunks + 2))
        def _():
            load_old(s - 2)
            send_near(s - 2)

        @pl.when(s == chunks + 1)
        def _():
            for d in range(2):
                first_copy(d).start()

        @pl.when(s >= 3)
        def _():
            finish(s - 3)

    for c in (chunks - 2, chunks - 1):
        for q in range(2):
            far_copy(c, q).wait_send()
            near_copy(c, q).wait_send()
        wait_outputs(c)
    for u in range(count):
        wait_for(other[u], other_recv.at[u])
    for d in range(2):
        first_copy(d).wait()


def reduce_and_step(chips, parts, terms, weights, ms, vs):
    layers = terms[0].shape[1]
    chunks = 3 * layers * 2
    blocks = [jax.ShapeDtypeStruct((size, *ms[i].shape[1:]), jnp.bfloat16) for i, _, size in parts]
    rows, columns = min(m.shape[1] for m in ms), min(m.shape[2] for m in ms)
    bf, f32 = jnp.bfloat16, jnp.float32
    tile = (rows, columns)
    dma = pltpu.SemaphoreType.DMA
    out = pl.pallas_call(
        functools.partial(reduce_kernel, chips, layers, parts),
        out_shape=blocks * 2 + [jax.ShapeDtypeStruct(m.shape, bf) for m in ms] + blocks[:1] * 2,
        in_specs=[pl.BlockSpec(memory_space=pl.ANY)] * 12,
        out_specs=[pl.BlockSpec(memory_space=pl.ANY)] * (2 * len(parts) + 5),
        scratch_shapes=[
            pltpu.VMEM((4, 4, 2, *tile), bf),
            pltpu.VMEM((4, 4, 2, *tile), bf),
            pltpu.VMEM((2, 2, *tile), f32),
            pltpu.VMEM((2, 2, *tile), f32),
            pltpu.VMEM((2, 2, *tile), bf),
            pltpu.VMEM((2, 2, *tile), bf),
            pltpu.VMEM((2, 2, *tile), bf),
            pltpu.VMEM((2, 2, *tile), bf),
            pltpu.VMEM((2, 2, 2, *tile), bf),
            pltpu.VMEM((chunks, 2, *tile), bf),
            pltpu.VMEM((chunks, 2, 2, *tile), bf),
            dma((4, 2)),
            dma((4, 2)),
            dma((4, 2)),
            dma((2, 3)),
            dma((2, 2, 2)),
            dma((2, 2)),
            dma((chunks, 2)),
            dma((2, 2)),
            dma((chunks, 2)),
            dma((2, 2)),
            dma((len(parts),)),
            dma((2,)),
            dma((2,)),
            pltpu.SemaphoreType.REGULAR,
        ],
        compiler_params=pltpu.CompilerParams(collective_id=0, has_side_effects=True, vmem_limit_bytes=67_000_000),
        name="reduce",
    )(*terms, *weights, *ms, *vs)
    count = len(parts)
    return out[:count], out[count : 2 * count], list(out[2 * count : 2 * count + 3]), out[-2:]


def place_kernel(chips, jobs, *refs):
    out, buf, in_sem, out_sem = refs[-4:]
    me = lax.axis_index("dp")
    x, k = me // CORES, lax.rem(me, CORES)
    copies = []
    for i, (layer, layers, rows, step, at, block_rows, other) in enumerate(jobs):
        block = lax.rem(x + step, chips) * CORES + (1 - k if other else k)
        slot = buf.at[i, pl.ds(0, layers), pl.ds(0, rows)]
        into = out.at[pl.ds(layer, layers), pl.ds(pl.multiple_of(block * block_rows + at, 8), rows)]
        copies.append((pltpu.make_async_copy(refs[i], slot, in_sem.at[i]), pltpu.make_async_copy(slot, into, out_sem.at[i])))
        copies[i][0].start()
    for first, second in copies:
        first.wait()
        second.start()
    for _, second in copies:
        second.wait()


def place(chips, shape, pieces, so_far):
    arrays = [p[0] for p in pieces]
    jobs = [(p[1], *p[0].shape[:2], *p[2:]) for p in pieces]
    size = max(a.shape[0] for a in arrays), max(a.shape[1] for a in arrays), arrays[0].shape[2]
    extra = () if so_far is None else (so_far,)
    return pl.pallas_call(
        functools.partial(place_kernel, chips, jobs),
        out_shape=jax.ShapeDtypeStruct(shape, jnp.bfloat16),
        in_specs=[pl.BlockSpec(memory_space=pl.ANY)] * (len(jobs) + len(extra)),
        out_specs=pl.BlockSpec(memory_space=pl.ANY),
        scratch_shapes=[
            pltpu.VMEM((len(jobs), *size), jnp.bfloat16),
            pltpu.SemaphoreType.DMA((len(jobs),)),
            pltpu.SemaphoreType.DMA((len(jobs),)),
        ],
        input_output_aliases={len(jobs): 0} if extra else {},
        compiler_params=pltpu.CompilerParams(vmem_limit_bytes=67_000_000),
        cost_estimate=pl.CostEstimate(flops=20_000_000, bytes_accessed=4 * sum(a.size for a in arrays), transcendentals=0),
        name="place",
    )(*arrays, *extra)


def solution(mesh):
    n = mesh.shape["dp"]
    chips = n // CORES

    def pairs(step, flip=0):
        return [(x * CORES + k, (x + step) % chips * CORES + (k + flip) % CORES) for x in range(chips) for k in range(CORES)]

    right, left, partner = pairs(1), pairs(-1), pairs(0, 1)

    def send(a, where):
        return lax.ppermute(a, "dp", where)

    def step(*arrays):
        terms, weights, ms, vs = (arrays[i : i + 3] for i in (0, 3, 6, 9))
        layers = terms[0].shape[1]
        f32 = jnp.float32
        parts = [(i, 0, layers) for i in range(2)] + [(2, layer, 1) for layer in range(layers)]
        fresh, other, gradients, first = reduce_and_step(chips, parts, terms, weights, ms, vs)

        last = len(parts) - 1
        whole, new_m, new_v = [None] * 3, [None] * 3, [None] * 3
        near, far, cuts = {0: first}, {}, {}
        for at, (i, start, size) in enumerate(parts):
            if at:
                near[at] = send(fresh[at], right), send(fresh[at], left)
            a, b = near[at]
            by_layer = size % 2 == 0
            half = (size if by_layer else a.shape[1]) // 2
            c, d = (a[:half], b[half:]) if by_layer else (a[:, :half], b[:, half:])
            cuts[at] = (start, 0), (start + half, 0) if by_layer else (start, half)
            far[at] = send(c, right), send(d, left)

        def put(at, pieces, apart=False):
            i = parts[at][0]
            rows = fresh[at].shape[1]
            theirs = [send(a, partner) if p is None else p for a, p, *_ in pieces]
            mine = [(p[0], *p[2:], rows, False) for p in pieces]
            theirs = [(t, *p[2:], rows, True) for t, p in zip(theirs, pieces)]
            if apart:
                whole[i] = place(chips, weights[i].shape, mine, whole[i])
                mine = []
            whole[i] = place(chips, weights[i].shape, mine + theirs, whole[i])

        for w in range(1, 3):
            c, d = far[w - 1]
            gradients[w], c = lax.optimization_barrier((gradients[w], c))
            far[w - 1] = c, d

        def put_far(at, apart=False):
            (c, d), ((c_layer, c_row), (d_layer, d_row)) = far[at], cuts[at]
            put(at, [(c, None, c_layer, 2, c_row), (d, None, d_layer, 2, d_row)], apart)

        for at, (i, start, _) in enumerate(parts):
            a, b = near[at]
            put(at, [(fresh[at], other[at], start, 0, 0), (a, None, start, chips - 1, 0), (b, None, start, 1, 0)])
            if at:
                put_far(at - 1)
        put_far(last, apart=True)
        for w in range(3):
            g = gradients[w].astype(f32)
            new_m[w] = 0.9 * ms[w] + 0.1 * g
            new_v[w] = 0.95 * vs[w] + 0.05 * g * g
        return (*whole, *new_m, *new_v)

    all_of, cut = P(None, None, None), P(None, "dp", None)
    return jax.shard_map(
        step,
        mesh=mesh,
        in_specs=(P(("rep", "dp"), None, None, None),) * 3 + (all_of,) * 3 + (cut,) * 6,
        out_specs=(P("rep", None, None),) * 3 + (P("rep", "dp", None),) * 6,
        check_vma=False,
    )
```

profile of v0, /device:TPU:113, one launch (start us, length us, event | category | flops | bytes accessed | tf_op | source)
XLA Modules:
  0.0 591.4 jit_solution(3589106817111197214)
XLA Ops:
  0.6 321.9 %reduce.1 = (bf16[2,144,4608]{2,1,0:T(8,128)(2,1)}, bf16[2,144,4608]{2,1,0:T(8,128)(2,1)}, bf16[1,576,1152]{2,1,0:T(8,128)(2,1)}, bf16[1,576,1152]{2,1,0:T(8,128...) custom-call(bf16[1,2,1152,4608]{3,2,1,0:T(8,128)(2,1)} %refs_0_.1, ...), custom_call_target="tpu_custom_call" | custom-call | tf_op jit(solution)/shard_map/reduce/pallas_call | solution.py:282
  322.6 1.1 collective-permute-start.20
  323.7 1.6 collective-permute-start.22
  325.3 2.7 collective-permute-start.17
  328.0 1.6 slice.24
  329.7 1.7 slice.25
  331.4 22.6 %collective-permute-done.20.refs_1_ = bf16[1,576,1152]{2,1,0:T(8,128)(2,1)S(1)} collective-permute-done((bf16[1,576,1152]{2,1,0:T(8,128)(2,1)}, bf16[1,576,1152]{2,1,0:T(8,128)(2,1)S(1)}, u32[]{:S(2)}, u32[]{:S(2)}) %collective-permute-start.20) | collective-permute-done | bytes 1327136 | tf_op jit(solution)/shard_map/ppermute | solution.py:371
  354.1 1.1 collective-permute-start.1
  355.1 3.0 collective-permute-start.28
  358.2 24.3 %collective-permute-done.14.refs_1_ = bf16[1,576,1152]{2,1,0:T(8,128)(2,1)S(1)} collective-permute-done((bf16[1,576,1152]{2,1,0:T(8,128)(2,1)}, bf16[1,576,1152]{2,1,0:T(8,128)(2,1)S(1)}, u32[]{:S(2)}, u32[]{:S(2)}) %collective-permute-start.14) | collective-permute-done | bytes 1327136 | tf_op jit(solution)/shard_map/ppermute | solution.py:371
  382.6 2.8 collective-permute-start.23
  385.4 25.7 %collective-permute-done.refs_0_ = bf16[1,144,4608]{2,1,0:T(8,128)(2,1)} collective-permute-done((bf16[1,144,4608]{2,1,0:T(8,128)(2,1)S(1)}, bf16[1,144,4608]{2,1,0:T(8,128)(2,1)}, u32[]{:S(2)}, u32[]{:S(2)}) %collective-permute-start) | collective-permute-done | bytes 1327136 | tf_op jit(solution)/shard_map/ppermute | solution.py:371
  411.1 2.8 collective-permute-start.18
  413.9 11.3 %collective-permute-done.21.refs_0_ = bf16[1,288,1152]{2,1,0:T(8,128)(2,1)S(1)} collective-permute-done((bf16[1,288,1152]{2,1,0:T(8,128)(2,1)S(1)}, bf16[1,288,1152]{2,1,0:T(8,128)(2,1)S(1)}, u32[]{:S(2)}, u32[]{:S(2)}) %collective-permute-start.21) | collective-permute-done | bytes 663584 | tf_op jit(solution)/shard_map/ppermute | solution.py:371
  425.2 2.7 collective-permute-start.29
  428.0 11.5 %collective-permute-done.15.refs_0_ = bf16[1,288,1152]{2,1,0:T(8,128)(2,1)} collective-permute-done((bf16[1,288,1152]{2,1,0:T(8,128)(2,1)S(1)}, bf16[1,288,1152]{2,1,0:T(8,128)(2,1)}, u32[]{:S(2)}, u32[]{:S(2)}) %collective-permute-start.15) | collective-permute-done | bytes 663584 | tf_op jit(solution)/shard_map/ppermute | solution.py:371
  439.5 1.1 collective-permute-start.8
  440.6 3.0 collective-permute-start.26
  443.7 0.4 collective-permute-start.24
  444.1 2.2 collective-permute-done.26.refs_4_
  446.3 0.4 collective-permute-start.4
  446.6 1.5 collective-permute-done.27.refs_5_
  448.2 0.4 collective-permute-start.5
  448.5 0.6 collective-permute-done.24.refs_2_
  449.1 0.4 collective-permute-start.25
  449.5 8.2 %collective-permute-done.25.refs_3_ = bf16[1,288,1152]{2,1,0:T(8,128)(2,1)S(1)} collective-permute-done((bf16[1,288,1152]{2,1,0:T(8,128)(2,1)S(1)}, bf16[1,288,1152]{2,1,0:T(8,128)(2,1)S(1)}, u32[]{:S(2)}, u32[]{:S(2)}) %collective-permute-start.25) | collective-permute-done | bytes 663584 | tf_op jit(solution)/shard_map/ppermute | solution.py:371
  457.6 0.4 collective-permute-start.2
  458.0 38.3 %collective-permute-done.6.refs_1_ = bf16[2,144,4608]{2,1,0:T(8,128)(2,1)} collective-permute-done((bf16[2,144,4608]{2,1,0:T(8,128)(2,1)S(1)}, bf16[2,144,4608]{2,1,0:T(8,128)(2,1)}, u32[]{:S(2)}, u32[]{:S(2)}) %collective-permute-start.6) | collective-permute-done | bytes 2654240 | tf_op jit(solution)/shard_map/ppermute | solution.py:371
  496.4 1.6 collective-permute-start.16
  497.9 1.6 collective-permute-start.19
  499.6 9.2 %fusion.3 = (f32[2,144,4608]{2,1,0:T(8,128)}, f32[2,144,4608]{2,1,0:T(8,128)}) fusion(bf16[2,144,4608]{2,1,0:T(8,128)(2,1)} %get-tuple-element.40, f32[2,144,4608]{2,1,0:T(8,128)} %refs_9_.1, f32[2,144,4608]{2,1,0:T(8,128)S(1)} %bitcast.1), kind=kLoop, calls=%fused_computation.9 | loop fusion | flops 10616832 | bytes 23887872 | tf_op jit(solution)/shard_map/add | solution.py:422
  508.8 2.6 slice.32
  511.4 2.5 slice.33
  514.0 2.6 collective-permute-start.9
  516.7 1.0 collective-permute-start.12
  517.7 10.1 %fusion.4 = (f32[2,144,4608]{2,1,0:T(8,128)}, f32[2,144,4608]{2,1,0:T(8,128)}) fusion(bf16[2,144,4608]{2,1,0:T(8,128)(2,1)S(1)} %copy-done.5, f32[2,144,4608]{2,1,0:T(8,128)} %refs_10_.1, f32[2,144,4608]{2,1,0:T(8,128)} %refs_7_.1), kind=kLoop, calls=%fused_computation.10 | loop fusion | flops 10616832 | bytes 23887872 | tf_op jit(solution)/shard_map/add | solution.py:422
  527.9 6.4 %place.13.refs_6_ = bf16[2,4608,1152]{2,1,0:T(8,128)(2,1)} custom-call(bf16[1,576,1152]{2,1,0:T(8,128)(2,1)} %get-tuple-element.37.refs_0_, bf16[1,576,1152]{2,1,0:T(8,128)(2,1)} %copy-done.1, bf16[1,576,1152]{2,1,0:T(8,128)(2,1)} %copy-done.3, bf16[1,576,1152]{2,1,0:T(8,128)(2,1)} %get-tuple-element.39.refs_3_, bf16[1,576,1152]{2,1,0:T(8,128)(2,1)} %copy-done.7, ...), custom_call_target="tpu_custom_call" | custom-call | flops 20000000 | bytes 15925248 | tf_op jit(solution)/shard_map/place/pallas_call | solution.py:344
  534.2 6.4 %place.14.refs_4_ = bf16[2,4608,1152]{2,1,0:T(8,128)(2,1)} custom-call(bf16[1,576,1152]{2,1,0:T(8,128)(2,1)} %get-tuple-element.36.refs_0_, bf16[1,576,1152]{2,1,0:T(8,128)(2,1)} %copy-done.2, bf16[1,576,1152]{2,1,0:T(8,128)(2,1)} %copy-done.4, bf16[1,576,1152]{2,1,0:T(8,128)(2,1)} %get-tuple-element.38.refs_3_, ...), custom_call_target="tpu_custom_call", output_to_operand_aliasing={{}: (6, {})} | custom-call | flops 20000000 | bytes 15925248 | tf_op jit(solution)/shard_map/place/pallas_call | solution.py:344
  540.6 2.7 place.15.refs_2_
  543.3 2.2 place.16.refs_2_
  545.5 2.2 place.17
  547.7 12.0 %place.9.refs_4_ = bf16[2,1152,4608]{2,1,0:T(8,128)(2,1)} custom-call(bf16[2,144,4608]{2,1,0:T(8,128)(2,1)} %get-tuple-element.30.refs_0_, bf16[2,144,4608]{2,1,0:T(8,128)(2,1)} %get-tuple-element.27.refs_1_, bf16[2,144,4608]{2,1,0:T(8,128)(2,1)} %get-tuple-element.29.refs_2_, bf16[2,144,4608]{2,1,0:T(8,128)(2,1)} %get-tuple-element.31.refs_3_, ...), custom_call_target="tpu_custom_call" | custom-call | flops 20000000 | bytes 31850496 | tf_op jit(solution)/shard_map/place/pallas_call | solution.py:344
  559.7 4.3 place.10
  564.0 0.5 collective-permute-start.10
  564.5 0.1 collective-permute-start.11
  564.6 10.5 %fusion.5 = (f32[2,576,1152]{2,1,0:T(8,128)}, f32[2,576,1152]{2,1,0:T(8,128)}) fusion(bf16[2,576,1152]{2,1,0:T(8,128)(2,1)} %get-tuple-element.42, f32[2,576,1152]{2,1,0:T(8,128)} %refs_11_.1, f32[2,576,1152]{2,1,0:T(8,128)} %refs_8_.1), kind=kLoop, calls=%fused_computation.11 | loop fusion | flops 10616832 | bytes 23887872 | tf_op jit(solution)/shard_map/add | solution.py:422
  575.1 12.0 %place.11.refs_4_ = bf16[2,1152,4608]{2,1,0:T(8,128)(2,1)} custom-call(bf16[2,144,4608]{2,1,0:T(8,128)(2,1)} %get-tuple-element.33.refs_0_, bf16[2,144,4608]{2,1,0:T(8,128)(2,1)} %collective-permute-done.6.refs_1_, bf16[2,144,4608]{2,1,0:T(8,128)(2,1)} %collective-permute-done.8.refs_2_, bf16[2,144,4608]{2,1,0:T(8,128)(2,1)} %get-tuple-element.35.refs_3_, ...), custom_call_target="tpu_custom_call" | custom-call | flops 20000000 | bytes 31850496 | tf_op jit(solution)/shard_map/place/pallas_call | solution.py:344
  587.1 4.3 place.12
  (68 shorter events, 0.8 us)
Async XLA Ops:
  322.6 177.0 %slice-start = ((s8[5308416]{0:T(1024)(128)(4,1)}), s8[4194304]{0:T(1024)(128)(4,1)S(1)}, s32[]{:S(2)}) async-start(s8[5308416]{0:T(1024)(128)(4,1)} %bitcast), calls=%async_computation | async-start | bytes 8388608
  322.6 31.5 %collective-permute-start.20 = (bf16[1,576,1152]{2,1,0:T(8,128)(2,1)}, bf16[1,576,1152]{2,1,0:T(8,128)(2,1)S(1)}, u32[]{:S(2)}, u32[]{:S(2)}) collective-permute-start(bf16[1,576,1152]{2,1,0:T(8,128)(2,1)} %get-tuple-element.37.refs_0_), channel_id=1, source_target_pairs={{0,2},{1,3},{2,4},{3,5},{4,6},{5,7},{6,0},{7,1},{8,10},{9,11},{10,... | collective-permute-start | bytes 3981320 | tf_op jit(solution)/shard_map/ppermute | solution.py:371
  323.7 31.4 %collective-permute-start.22 = (bf16[1,576,1152]{2,1,0:T(8,128)(2,1)}, bf16[1,576,1152]{2,1,0:T(8,128)(2,1)S(1)}, u32[]{:S(2)}, u32[]{:S(2)}) collective-permute-start(bf16[1,576,1152]{2,1,0:T(8,128)(2,1)} %get-tuple-element.37.refs_0_), channel_id=1, source_target_pairs={{0,6},{1,7},{2,0},{3,1},{4,2},{5,3},{6,4},{7,5},{8,14},{9,15},{10,... | collective-permute-start | bytes 3981320 | tf_op jit(solution)/shard_map/ppermute | solution.py:371
  325.3 57.2 %collective-permute-start.14 = (bf16[1,576,1152]{2,1,0:T(8,128)(2,1)}, bf16[1,576,1152]{2,1,0:T(8,128)(2,1)S(1)}, u32[]{:S(2)}, u32[]{:S(2)}) collective-permute-start(bf16[1,576,1152]{2,1,0:T(8,128)(2,1)} %get-tuple-element.36.refs_0_), channel_id=1, source_target_pairs={{0,2},{1,3},{2,4},{3,5},{4,6},{5,7},{6,0},{7,1},{8,10},{9,11},{10,... | collective-permute-start | bytes 3981320 | tf_op jit(solution)/shard_map/ppermute | solution.py:371
  325.3 57.2 %collective-permute-start.17 = (bf16[1,576,1152]{2,1,0:T(8,128)(2,1)}, bf16[1,576,1152]{2,1,0:T(8,128)(2,1)S(1)}, u32[]{:S(2)}, u32[]{:S(2)}) collective-permute-start(bf16[1,576,1152]{2,1,0:T(8,128)(2,1)} %get-tuple-element.36.refs_0_), channel_id=1, source_target_pairs={{0,6},{1,7},{2,0},{3,1},{4,2},{5,3},{6,4},{7,5},{8,14},{9,15},{10,... | collective-permute-start | bytes 3981320 | tf_op jit(solution)/shard_map/ppermute | solution.py:371
  328.0 99.9 %copy-start.6 = (bf16[2,144,4608]{2,1,0:T(8,128)(2,1)S(1)}, bf16[2,144,4608]{2,1,0:T(8,128)(2,1)}, u32[]{:S(2)}) copy-start(bf16[2,144,4608]{2,1,0:T(8,128)(2,1)} %get-tuple-element.33.refs_0_) | copy-start | bytes 7962628
  328.0 118.2 %copy-start = (bf16[2,144,4608]{2,1,0:T(8,128)(2,1)S(1)}, bf16[2,144,4608]{2,1,0:T(8,128)(2,1)}, u32[]{:S(2)}) copy-start(bf16[2,144,4608]{2,1,0:T(8,128)(2,1)} %get-tuple-element.27.refs_1_) | copy-start | bytes 7962628
  329.6 81.5 %collective-permute-start = (bf16[1,144,4608]{2,1,0:T(8,128)(2,1)S(1)}, bf16[1,144,4608]{2,1,0:T(8,128)(2,1)}, u32[]{:S(2)}, u32[]{:S(2)}) collective-permute-start(bf16[1,144,4608]{2,1,0:T(8,128)(2,1)S(1)} %slice.24), channel_id=1, source_target_pairs={{0,2},{1,3},{2,4},{3,5},{4,6},{5,7},{6,0},{7,1},{8,10},{9,11},{10,... | collective-permute-start | bytes 3981320 | tf_op jit(solution)/shard_map/ppermute | solution.py:371
  329.7 169.9 %slice-start.1 = ((s8[5308416]{0:T(1024)(128)(4,1)}), s8[1114112]{0:T(1024)(128)(4,1)S(1)}, s32[]{:S(2)}) async-start(s8[5308416]{0:T(1024)(128)(4,1)} %bitcast), calls=%async_computation.1 | async-start | bytes 2228224
  354.1 92.6 %copy-start.1 = (bf16[1,576,1152]{2,1,0:T(8,128)(2,1)}, bf16[1,576,1152]{2,1,0:T(8,128)(2,1)S(1)}, u32[]{:S(2)}) copy-start(bf16[1,576,1152]{2,1,0:T(8,128)(2,1)S(1)} %collective-permute-done.20.refs_1_) | copy-start | bytes 3981316
  354.1 57.0 %collective-permute-start.1 = (bf16[1,144,4608]{2,1,0:T(8,128)(2,1)S(1)}, bf16[1,144,4608]{2,1,0:T(8,128)(2,1)}, u32[]{:S(2)}, u32[]{:S(2)}) collective-permute-start(bf16[1,144,4608]{2,1,0:T(8,128)(2,1)S(1)} %slice.25), channel_id=1, source_target_pairs={{0,6},{1,7},{2,0},{3,1},{4,2},{5,3},{6,4},{7,5},{8,14},{9,15},{10,... | collective-permute-start | bytes 3981320 | tf_op jit(solution)/shard_map/ppermute | solution.py:371
  355.1 93.4 %copy-start.3 = (bf16[1,576,1152]{2,1,0:T(8,128)(2,1)}, bf16[1,576,1152]{2,1,0:T(8,128)(2,1)S(1)}, u32[]{:S(2)}) copy-start(bf16[1,576,1152]{2,1,0:T(8,128)(2,1)S(1)} %collective-permute-done.22.refs_2_) | copy-start | bytes 3981316
  355.1 88.4 %collective-permute-start.28 = (bf16[1,576,1152]{2,1,0:T(8,128)(2,1)S(1)}, bf16[1,576,1152]{2,1,0:T(8,128)(2,1)S(1)}, u32[]{:S(2)}, u32[]{:S(2)}) collective-permute-start(bf16[1,576,1152]{2,1,0:T(8,128)(2,1)S(1)} %collective-permute-done.20.refs_1_), channel_id=1, source_target_pairs={{0,1},{1,0},{2,3},{3,2},{4,5},{5,4},{6,7},{7,6},{8,9},{9,8},{10,11... | collective-permute-start | bytes 3981320 | tf_op jit(solution)/shard_map/ppermute | solution.py:371
  382.5 65.7 %copy-start.2 = (bf16[1,576,1152]{2,1,0:T(8,128)(2,1)}, bf16[1,576,1152]{2,1,0:T(8,128)(2,1)S(1)}, u32[]{:S(2)}) copy-start(bf16[1,576,1152]{2,1,0:T(8,128)(2,1)S(1)} %collective-permute-done.14.refs_1_) | copy-start | bytes 3981316
  382.5 42.7 %collective-permute-start.21 = (bf16[1,288,1152]{2,1,0:T(8,128)(2,1)S(1)}, bf16[1,288,1152]{2,1,0:T(8,128)(2,1)S(1)}, u32[]{:S(2)}, u32[]{:S(2)}) collective-permute-start(bf16[1,288,1152]{2,1,0:T(8,128)(2,1)S(1)} %slice.36), channel_id=1, source_target_pairs={{0,2},{1,3},{2,4},{3,5},{4,6},{5,7},{6,0},{7,1},{8,10},{9,11},{10,... | collective-permute-start | bytes 1990664 | tf_op jit(solution)/shard_map/ppermute | solution.py:371
  382.6 66.5 %copy-start.4 = (bf16[1,576,1152]{2,1,0:T(8,128)(2,1)}, bf16[1,576,1152]{2,1,0:T(8,128)(2,1)S(1)}, u32[]{:S(2)}) copy-start(bf16[1,576,1152]{2,1,0:T(8,128)(2,1)S(1)} %collective-permute-done.17.refs_2_) | copy-start | bytes 3981316
  382.6 45.3 %collective-permute-start.23 = (bf16[1,288,1152]{2,1,0:T(8,128)(2,1)S(1)}, bf16[1,288,1152]{2,1,0:T(8,128)(2,1)S(1)}, u32[]{:S(2)}, u32[]{:S(2)}) collective-permute-start(bf16[1,288,1152]{2,1,0:T(8,128)(2,1)S(1)} %slice.37), channel_id=1, source_target_pairs={{0,6},{1,7},{2,0},{3,1},{4,2},{5,3},{6,4},{7,5},{8,14},{9,15},{10,... | collective-permute-start | bytes 1990664 | tf_op jit(solution)/shard_map/ppermute | solution.py:371
  411.0 28.4 %collective-permute-start.15 = (bf16[1,288,1152]{2,1,0:T(8,128)(2,1)S(1)}, bf16[1,288,1152]{2,1,0:T(8,128)(2,1)}, u32[]{:S(2)}, u32[]{:S(2)}) collective-permute-start(bf16[1,288,1152]{2,1,0:T(8,128)(2,1)S(1)} %slice.34), channel_id=1, source_target_pairs={{0,2},{1,3},{2,4},{3,5},{4,6},{5,7},{6,0},{7,1},{8,10},{9,11},{10,... | collective-permute-start | bytes 1990664 | tf_op jit(solution)/shard_map/ppermute | solution.py:371
  411.1 29.4 %collective-permute-start.18 = (bf16[1,288,1152]{2,1,0:T(8,128)(2,1)S(1)}, bf16[1,288,1152]{2,1,0:T(8,128)(2,1)}, u32[]{:S(2)}, u32[]{:S(2)}) collective-permute-start(bf16[1,288,1152]{2,1,0:T(8,128)(2,1)S(1)} %slice.35), channel_id=1, source_target_pairs={{0,6},{1,7},{2,0},{3,1},{4,2},{5,3},{6,4},{7,5},{8,14},{9,15},{10,... | collective-permute-start | bytes 1990664 | tf_op jit(solution)/shard_map/ppermute | solution.py:371
  425.2 74.4 %copy-start.11 = (bf16[1,288,1152]{2,1,0:T(8,128)(2,1)}, bf16[1,288,1152]{2,1,0:T(8,128)(2,1)S(1)}, u32[]{:S(2)}) copy-start(bf16[1,288,1152]{2,1,0:T(8,128)(2,1)S(1)} %collective-permute-done.21.refs_0_) | copy-start | bytes 1990660
  425.2 18.5 %collective-permute-start.29 = (bf16[1,576,1152]{2,1,0:T(8,128)(2,1)S(1)}, bf16[1,576,1152]{2,1,0:T(8,128)(2,1)S(1)}, u32[]{:S(2)}, u32[]{:S(2)}) collective-permute-start(bf16[1,576,1152]{2,1,0:T(8,128)(2,1)S(1)} %collective-permute-done.22.refs_2_), channel_id=1, source_target_pairs={{0,1},{1,0},{2,3},{3,2},{4,5},{5,4},{6,7},{7,6},{8,9},{9,8},{10,11... | collective-permute-start | bytes 3981320 | tf_op jit(solution)/shard_map/ppermute | solution.py:371
  427.9 71.7 %copy-start.12 = (bf16[1,288,1152]{2,1,0:T(8,128)(2,1)}, bf16[1,288,1152]{2,1,0:T(8,128)(2,1)S(1)}, u32[]{:S(2)}) copy-start(bf16[1,288,1152]{2,1,0:T(8,128)(2,1)S(1)} %collective-permute-done.23.refs_1_) | copy-start | bytes 1990660
  427.9 68.5 %collective-permute-start.6 = (bf16[2,144,4608]{2,1,0:T(8,128)(2,1)S(1)}, bf16[2,144,4608]{2,1,0:T(8,128)(2,1)}, u32[]{:S(2)}, u32[]{:S(2)}) collective-permute-start(bf16[2,144,4608]{2,1,0:T(8,128)(2,1)S(1)} %copy-done.6), channel_id=1, source_target_pairs={{0,2},{1,3},{2,4},{3,5},{4,6},{5,7},{6,0},{7,1},{8,10},{9,11},{10,... | collective-permute-start | bytes 7962632 | tf_op jit(solution)/shard_map/ppermute | solution.py:371
  439.5 58.5 %collective-permute-start.8 = (bf16[2,144,4608]{2,1,0:T(8,128)(2,1)S(1)}, bf16[2,144,4608]{2,1,0:T(8,128)(2,1)}, u32[]{:S(2)}, u32[]{:S(2)}) collective-permute-start(bf16[2,144,4608]{2,1,0:T(8,128)(2,1)S(1)} %copy-done.6), channel_id=1, source_target_pairs={{0,6},{1,7},{2,0},{3,1},{4,2},{5,3},{6,4},{7,5},{8,14},{9,15},{10,... | collective-permute-start | bytes 7962632 | tf_op jit(solution)/shard_map/ppermute | solution.py:371
  440.6 5.7 collective-permute-start.26
  443.6 54.4 %copy-start.7 = (bf16[1,576,1152]{2,1,0:T(8,128)(2,1)}, bf16[1,576,1152]{2,1,0:T(8,128)(2,1)S(1)}, u32[]{:S(2)}) copy-start(bf16[1,576,1152]{2,1,0:T(8,128)(2,1)S(1)} %collective-permute-done.28.refs_4_) | copy-start | bytes 3981316
  443.6 4.6 collective-permute-start.27
  443.7 55.9 %copy-start.8 = (bf16[1,576,1152]{2,1,0:T(8,128)(2,1)}, bf16[1,576,1152]{2,1,0:T(8,128)(2,1)S(1)}, u32[]{:S(2)}) copy-start(bf16[1,576,1152]{2,1,0:T(8,128)(2,1)S(1)} %collective-permute-done.29.refs_5_) | copy-start | bytes 3981316
  443.7 5.4 collective-permute-start.24
  446.3 53.3 %copy-start.9 = (bf16[1,576,1152]{2,1,0:T(8,128)(2,1)}, bf16[1,576,1152]{2,1,0:T(8,128)(2,1)S(1)}, u32[]{:S(2)}) copy-start(bf16[1,576,1152]{2,1,0:T(8,128)(2,1)S(1)} %collective-permute-done.26.refs_4_) | copy-start | bytes 3981316
  446.3 67.8 %collective-permute-start.4 = (bf16[2,144,4608]{2,1,0:T(8,128)(2,1)S(1)}, bf16[2,144,4608]{2,1,0:T(8,128)(2,1)}, u32[]{:S(2)}, u32[]{:S(2)}) collective-permute-start(bf16[2,144,4608]{2,1,0:T(8,128)(2,1)S(1)} %copy-done), channel_id=1, source_target_pairs={{0,1},{1,0},{2,3},{3,2},{4,5},{5,4},{6,7},{7,6},{8,9},{9,8},{10,11... | collective-permute-start | bytes 7962632 | tf_op jit(solution)/shard_map/ppermute | solution.py:371
  448.2 51.4 %copy-start.10 = (bf16[1,576,1152]{2,1,0:T(8,128)(2,1)}, bf16[1,576,1152]{2,1,0:T(8,128)(2,1)S(1)}, u32[]{:S(2)}) copy-start(bf16[1,576,1152]{2,1,0:T(8,128)(2,1)S(1)} %collective-permute-done.27.refs_5_) | copy-start | bytes 3981316
  448.2 68.5 %collective-permute-start.5 = (bf16[2,144,4608]{2,1,0:T(8,128)(2,1)}, bf16[2,144,4608]{2,1,0:T(8,128)(2,1)}, u32[]{:S(2)}, u32[]{:S(2)}) collective-permute-start(bf16[2,144,4608]{2,1,0:T(8,128)(2,1)} %get-tuple-element.29.refs_2_), channel_id=1, source_target_pairs={{0,1},{1,0},{2,3},{3,2},{4,5},{5,4},{6,7},{7,6},{8,9},{9,8},{10,11... | collective-permute-start | bytes 7962632 | tf_op jit(solution)/shard_map/ppermute | solution.py:371
  449.1 50.5 %copy-start.13 = (bf16[1,288,1152]{2,1,0:T(8,128)(2,1)}, bf16[1,288,1152]{2,1,0:T(8,128)(2,1)S(1)}, u32[]{:S(2)}) copy-start(bf16[1,288,1152]{2,1,0:T(8,128)(2,1)S(1)} %collective-permute-done.24.refs_2_) | copy-start | bytes 1990660
  449.1 8.5 %collective-permute-start.25 = (bf16[1,288,1152]{2,1,0:T(8,128)(2,1)S(1)}, bf16[1,288,1152]{2,1,0:T(8,128)(2,1)S(1)}, u32[]{:S(2)}, u32[]{:S(2)}) collective-permute-start(bf16[1,288,1152]{2,1,0:T(8,128)(2,1)S(1)} %collective-permute-done.23.refs_1_), channel_id=1, source_target_pairs={{0,1},{1,0},{2,3},{3,2},{4,5},{5,4},{6,7},{7,6},{8,9},{9,8},{10,11... | collective-permute-start | bytes 1990664 | tf_op jit(solution)/shard_map/ppermute | solution.py:371
  457.6 42.0 %copy-start.14 = (bf16[1,288,1152]{2,1,0:T(8,128)(2,1)}, bf16[1,288,1152]{2,1,0:T(8,128)(2,1)S(1)}, u32[]{:S(2)}) copy-start(bf16[1,288,1152]{2,1,0:T(8,128)(2,1)S(1)} %collective-permute-done.25.refs_3_) | copy-start | bytes 1990660
  457.6 60.0 %collective-permute-start.2 = (bf16[1,144,4608]{2,1,0:T(8,128)(2,1)}, bf16[1,144,4608]{2,1,0:T(8,128)(2,1)}, u32[]{:S(2)}, u32[]{:S(2)}) collective-permute-start(bf16[1,144,4608]{2,1,0:T(8,128)(2,1)} %collective-permute-done.refs_0_), channel_id=1, source_target_pairs={{0,1},{1,0},{2,3},{3,2},{4,5},{5,4},{6,7},{7,6},{8,9},{9,8},{10,11... | collective-permute-start | bytes 3981320 | tf_op jit(solution)/shard_map/ppermute | solution.py:371
  496.4 17.5 %collective-permute-start.16 = (bf16[1,288,1152]{2,1,0:T(8,128)(2,1)}, bf16[1,288,1152]{2,1,0:T(8,128)(2,1)}, u32[]{:S(2)}, u32[]{:S(2)}) collective-permute-start(bf16[1,288,1152]{2,1,0:T(8,128)(2,1)} %collective-permute-done.15.refs_0_), channel_id=1, source_target_pairs={{0,1},{1,0},{2,3},{3,2},{4,5},{5,4},{6,7},{7,6},{8,9},{9,8},{10,11... | collective-permute-start | bytes 1990664 | tf_op jit(solution)/shard_map/ppermute | solution.py:371
  497.9 16.0 %collective-permute-start.19 = (bf16[1,288,1152]{2,1,0:T(8,128)(2,1)}, bf16[1,288,1152]{2,1,0:T(8,128)(2,1)}, u32[]{:S(2)}, u32[]{:S(2)}) collective-permute-start(bf16[1,288,1152]{2,1,0:T(8,128)(2,1)} %collective-permute-done.18.refs_1_), channel_id=1, source_target_pairs={{0,1},{1,0},{2,3},{3,2},{4,5},{5,4},{6,7},{7,6},{8,9},{9,8},{10,11... | collective-permute-start | bytes 1990664 | tf_op jit(solution)/shard_map/ppermute | solution.py:371
  508.8 8.9 %copy-start.5 = (bf16[2,144,4608]{2,1,0:T(8,128)(2,1)S(1)}, bf16[2,144,4608]{2,1,0:T(8,128)(2,1)}, u32[]{:S(2)}) copy-start(bf16[2,144,4608]{2,1,0:T(8,128)(2,1)} %get-tuple-element.41) | copy-start | bytes 7962628
  513.9 45.8 %collective-permute-start.3 = (bf16[1,144,4608]{2,1,0:T(8,128)(2,1)}, bf16[1,144,4608]{2,1,0:T(8,128)(2,1)}, u32[]{:S(2)}, u32[]{:S(2)}) collective-permute-start(bf16[1,144,4608]{2,1,0:T(8,128)(2,1)} %collective-permute-done.1.refs_1_), channel_id=1, source_target_pairs={{0,1},{1,0},{2,3},{3,2},{4,5},{5,4},{6,7},{7,6},{8,9},{9,8},{10,11... | collective-permute-start | bytes 3981320 | tf_op jit(solution)/shard_map/ppermute | solution.py:371
  513.9 50.1 %collective-permute-start.7 = (bf16[1,144,4608]{2,1,0:T(8,128)(2,1)}, bf16[1,144,4608]{2,1,0:T(8,128)(2,1)}, u32[]{:S(2)}, u32[]{:S(2)}) collective-permute-start(bf16[1,144,4608]{2,1,0:T(8,128)(2,1)} %slice.32), channel_id=1, source_target_pairs={{0,2},{1,3},{2,4},{3,5},{4,6},{5,7},{6,0},{7,1},{8,10},{9,11},{10,... | collective-permute-start | bytes 3981320 | tf_op jit(solution)/shard_map/ppermute | solution.py:371
  514.0 50.5 %collective-permute-start.9 = (bf16[1,144,4608]{2,1,0:T(8,128)(2,1)}, bf16[1,144,4608]{2,1,0:T(8,128)(2,1)}, u32[]{:S(2)}, u32[]{:S(2)}) collective-permute-start(bf16[1,144,4608]{2,1,0:T(8,128)(2,1)} %slice.33), channel_id=1, source_target_pairs={{0,6},{1,7},{2,0},{3,1},{4,2},{5,3},{6,4},{7,5},{8,14},{9,15},{10,... | collective-permute-start | bytes 3981320 | tf_op jit(solution)/shard_map/ppermute | solution.py:371
  516.7 58.4 %collective-permute-start.12 = (bf16[2,144,4608]{2,1,0:T(8,128)(2,1)}, bf16[2,144,4608]{2,1,0:T(8,128)(2,1)}, u32[]{:S(2)}, u32[]{:S(2)}) collective-permute-start(bf16[2,144,4608]{2,1,0:T(8,128)(2,1)} %collective-permute-done.6.refs_1_), channel_id=1, source_target_pairs={{0,1},{1,0},{2,3},{3,2},{4,5},{5,4},{6,7},{7,6},{8,9},{9,8},{10,11... | collective-permute-start | bytes 7962632 | tf_op jit(solution)/shard_map/ppermute | solution.py:371
  517.7 57.4 %collective-permute-start.13 = (bf16[2,144,4608]{2,1,0:T(8,128)(2,1)}, bf16[2,144,4608]{2,1,0:T(8,128)(2,1)}, u32[]{:S(2)}, u32[]{:S(2)}) collective-permute-start(bf16[2,144,4608]{2,1,0:T(8,128)(2,1)} %collective-permute-done.8.refs_2_), channel_id=1, source_target_pairs={{0,1},{1,0},{2,3},{3,2},{4,5},{5,4},{6,7},{7,6},{8,9},{9,8},{10,11... | collective-permute-start | bytes 7962632 | tf_op jit(solution)/shard_map/ppermute | solution.py:371
  564.0 23.1 %collective-permute-start.10 = (bf16[1,144,4608]{2,1,0:T(8,128)(2,1)}, bf16[1,144,4608]{2,1,0:T(8,128)(2,1)}, u32[]{:S(2)}, u32[]{:S(2)}) collective-permute-start(bf16[1,144,4608]{2,1,0:T(8,128)(2,1)} %collective-permute-done.7.refs_0_), channel_id=1, source_target_pairs={{0,1},{1,0},{2,3},{3,2},{4,5},{5,4},{6,7},{7,6},{8,9},{9,8},{10,11... | collective-permute-start | bytes 3981320 | tf_op jit(solution)/shard_map/ppermute | solution.py:371
  564.5 22.6 %collective-permute-start.11 = (bf16[1,144,4608]{2,1,0:T(8,128)(2,1)}, bf16[1,144,4608]{2,1,0:T(8,128)(2,1)}, u32[]{:S(2)}, u32[]{:S(2)}) collective-permute-start(bf16[1,144,4608]{2,1,0:T(8,128)(2,1)} %collective-permute-done.9.refs_1_), channel_id=1, source_target_pairs={{0,1},{1,0},{2,3},{3,2},{4,5},{5,4},{6,7},{7,6},{8,9},{9,8},{10,11... | collective-permute-start | bytes 3981320 | tf_op jit(solution)/shard_map/ppermute | solution.py:371
where the time goes:
time: 592 us; the launch traced here: 591 us
  Pallas kernels  374 us (63%)
  waiting for transfers between devices  146 us (25%)
  starting transfers between devices  31.7 us (5%)
  other arithmetic  29.7 us (5%)
  local copies, waits for them, and re-layouts  8.63 us (1%)
    pallas_call x1, Pallas kernels, reduce_and_step(): pl.pallas_call(functools.partial(reduce_kernel, chips, layers, parts), ou...  322 us
    ppermute x30, waiting for transfers between devices, send(): return lax.ppermute(a, 'dp', where)  146 us
    pallas_call x9, Pallas kernels, place(): pl.pallas_call(functools.partial(place_kernel, chips, jobs), out_shape=ja...  52.4 us
    ppermute x30, starting transfers between devices, send(): return lax.ppermute(a, 'dp', where)  31.7 us
    add x3, other arithmetic, step(): new_v[w] = 0.95 * vs[w] + 0.05 * g * g  29.7 us
  transfers between devices with their start and end apart: 30, of which 10 were waited for; matrix products, arithmetic and copies ran while one was open for 6% of the time, Pallas kernels for 8%

commit v1 on v0

--- a/solution.py
+++ b/solution.py
@@ -11,6 +11,8 @@
 CORES = 2
 PIECES = 4
 STRIP = 16
+SLOTS = 4
+GROUPS = 3
 MESH = pl.DeviceIdType.MESH
 ORDER = (2, 1, 3, 0)
 
@@ -48,26 +50,34 @@
         for i in range(weights):
             pl.when(c // (layers * 2) == i)(functools.partial(body, i, lax.rem(c // 2, layers), lax.rem(c, 2)))
 
-    def load(c):
-        slot = lax.rem(c, 4)
+    def load(c, group, cuts):
+        slot = lax.rem(c, SLOTS)
+        size = rows // cuts
 
         def start(i, layer, h):
-            for group in ((0,), (1, 2, 3)):
-                late = min(group[0], 1)
+            for r in range(cuts):
+                at = pl.ds(r * size, size)
+                sem = r if 0 in group else GROUPS
                 for j in group:
                     block = lax.rem(x + ORDER[j], chips) * CORES
                     for q in range(2):
                         pltpu.make_async_remote_copy(
-                            src_ref=piece(terms[i], (0, layer), block + 1 - k, h * 2 + q),
-                            dst_ref=oth.at[slot, j, q],
-                            send_sem=oth_send.at[slot, late],
-                            recv_sem=oth_recv.at[slot, late],
+                            src_ref=piece(terms[i], (0, layer), block + 1 - k, h * 2 + q).at[at],
+                            dst_ref=oth.at[slot, j, q, at],
+                            send_sem=oth_send.at[slot, sem],
+                            recv_sem=oth_recv.at[slot, sem],
                             device_id=partner,
                             device_id_type=MESH,
                         ).start()
-                        pltpu.make_async_copy(piece(terms[i], (0, layer), block + k, h * 2 + q), own.at[slot, j, q], own_sem.at[slot, late]).start()
+                        pltpu.make_async_copy(piece(terms[i], (0, layer), block + k, h * 2 + q).at[at], own.at[slot, j, q, at], own_sem.at[slot, sem]).start()
 
         for_weight(c, start)
+
+    def load_far(c):
+        load(c, (0,), GROUPS)
+
+    def load_near(c):
+        load(c, (1, 2, 3), 1)
 
     def load_old(c):
         slot = lax.rem(c, 2)
@@ -84,24 +94,23 @@
     def wait_for(ref, sem):
         pltpu.make_async_copy(ref, ref, sem).wait()
 
-    def wait_terms(slot, late):
-        part = pl.ds(late, 3) if late else pl.ds(0, 1)
-        wait_for(own.at[slot, part], own_sem.at[slot, late])
-        wait_for(oth.at[slot, part], oth_recv.at[slot, late])
-        wait_for(oth.at[slot, part], oth_send.at[slot, late])
-
-    def strips(body):
-        @pl.loop(0, rows // STRIP)
+    def wait_terms(slot, part, at, sem):
+        wait_for(own.at[slot, part, :, at], own_sem.at[slot, sem])
+        wait_for(oth.at[slot, part, :, at], oth_recv.at[slot, sem])
+        wait_for(oth.at[slot, part, :, at], oth_send.at[slot, sem])
+
+    def strips(body, first=0, count=rows):
+        @pl.loop(0, count // STRIP)
         def _(r):
-            body(pl.ds(pl.multiple_of(r * STRIP, STRIP), STRIP))
+            body(pl.ds(pl.multiple_of(first + r * STRIP, STRIP), STRIP))
 
     def pair(slot, j, q, at):
         return own[slot, j, q, at].astype(jnp.float32) + oth[slot, j, q, at].astype(jnp.float32)
 
-    def far_copy(c, q):
+    def far_copy(c, q, at=pl.ds(0, rows)):
         return pltpu.make_async_remote_copy(
-            src_ref=far.at[lax.rem(c, 2), q],
-            dst_ref=from_far.at[c, q],
+            src_ref=far.at[lax.rem(c, 2), q, at],
+            dst_ref=from_far.at[c, q, at],
             send_sem=far_send.at[lax.rem(c, 2), q],
             recv_sem=far_recv.at[c, q],
             device_id=(right, left)[q],
@@ -119,8 +128,7 @@
         )
 
     def send_far(c):
-        slot = lax.rem(c, 4)
-        wait_terms(slot, 0)
+        slot = lax.rem(c, SLOTS)
 
         @pl.when(c >= 2)
         def _():
@@ -131,13 +139,17 @@
             for q in range(2):
                 far[lax.rem(c, 2), q, at] = pair(slot, 0, q, at).astype(far.dtype)
 
-        strips(strip)
-        for q in range(2):
-            far_copy(c, q).start()
+        size = rows // GROUPS
+        for r in range(GROUPS):
+            at = pl.ds(r * size, size)
+            wait_terms(slot, pl.ds(0, 1), at, r)
+            strips(strip, r * size, size)
+            for q in range(2):
+                far_copy(c, q, at).start()
 
     def send_near(c):
-        slot = lax.rem(c, 4)
-        wait_terms(slot, 1)
+        slot = lax.rem(c, SLOTS)
+        wait_terms(slot, pl.ds(1, 3), pl.ds(0, rows), GROUPS)
 
         @pl.when(c >= 2)
         def _():
@@ -197,12 +209,12 @@
             dst_ref=first[d],
             send_sem=first_send.at[d],
             recv_sem=first_recv.at[d],
-            device_id=(right, left)[d],
+            device_id={"dp": lax.rem(x + (chips - 1 if d else 1) * (1 - 2 * k) + chips, chips) * CORES + k},
             device_id_type=MESH,
         )
 
     def finish(c):
-        slot, two = lax.rem(c, 4), lax.rem(c, 2)
+        slot, two = lax.rem(c, SLOTS), lax.rem(c, 2)
         wait_for(m_in.at[two], old_sem.at[two, 0])
         wait_for(v_in.at[two], old_sem.at[two, 1])
         wait_for(w_in.at[two], old_sem.at[two, 2])
@@ -228,7 +240,7 @@
         strips(strip)
         start_outputs(c)
 
-        @pl.when(c + 4 < chunks)
+        @pl.when(c + SLOTS < chunks)
         def _():
             pl.semaphore_signal(free_sem, inc=1, device_id=partner, device_id_type=MESH)
 
@@ -237,21 +249,22 @@
         @pl.when((s >= 1) & (s < chunks + 1))
         def _():
             send_far(s - 1)
+            load_near(s - 1)
 
         @pl.when(s < chunks)
         def _():
-            @pl.when(s >= 4)
+            @pl.when(s >= SLOTS)
             def _():
                 pl.semaphore_wait(free_sem, 1)
 
-            load(s)
+            load_far(s)
 
         @pl.when((s >= 2) & (s < chunks + 2))
         def _():
             load_old(s - 2)
             send_near(s - 2)
 
-        @pl.when(s == chunks + 1)
+        @pl.when((s == chunks + 1) & (k == 0))
         def _():
             for d in range(2):
                 first_copy(d).start()
@@ -265,6 +278,12 @@
             far_copy(c, q).wait_send()
             near_copy(c, q).wait_send()
         wait_outputs(c)
+
+    @pl.when(k != 0)
+    def _():
+        for d in range(2):
+            first_copy(d).start()
+
     for u in range(count):
         wait_for(other[u], other_recv.at[u])
     for d in range(2):
@@ -285,8 +304,8 @@
         in_specs=[pl.BlockSpec(memory_space=pl.ANY)] * 12,
         out_specs=[pl.BlockSpec(memory_space=pl.ANY)] * (2 * len(parts) + 5),
         scratch_shapes=[
-            pltpu.VMEM((4, 4, 2, *tile), bf),
-            pltpu.VMEM((4, 4, 2, *tile), bf),
+            pltpu.VMEM((SLOTS, 4, 2, *tile), bf),
+            pltpu.VMEM((SLOTS, 4, 2, *tile), bf),
             pltpu.VMEM((2, 2, *tile), f32),
             pltpu.VMEM((2, 2, *tile), f32),
             pltpu.VMEM((2, 2, *tile), bf),
@@ -296,9 +315,9 @@
             pltpu.VMEM((2, 2, 2, *tile), bf),
             pltpu.VMEM((chunks, 2, *tile), bf),
             pltpu.VMEM((chunks, 2, 2, *tile), bf),
-            dma((4, 2)),
-            dma((4, 2)),
-            dma((4, 2)),
+            dma((SLOTS, GROUPS + 1)),
+            dma((SLOTS, GROUPS + 1)),
+            dma((SLOTS, GROUPS + 1)),
             dma((2, 3)),
             dma((2, 2, 2)),
             dma((2, 2)),
@@ -324,7 +343,8 @@
     x, k = me // CORES, lax.rem(me, CORES)
     copies = []
     for i, (layer, layers, rows, step, at, block_rows, other) in enumerate(jobs):
-        block = lax.rem(x + step, chips) * CORES + (1 - k if other else k)
+        core = 1 - k if other else k
+        block = lax.rem(x + step * (1 - 2 * core) + chips, chips) * CORES + core
         slot = buf.at[i, pl.ds(0, layers), pl.ds(0, rows)]
         into = out.at[pl.ds(layer, layers), pl.ds(pl.multiple_of(block * block_rows + at, 8), rows)]
         copies.append((pltpu.make_async_copy(refs[i], slot, in_sem.at[i]), pltpu.make_async_copy(slot, into, out_sem.at[i])))
@@ -363,9 +383,9 @@
     chips = n // CORES
 
     def pairs(step, flip=0):
-        return [(x * CORES + k, (x + step) % chips * CORES + (k + flip) % CORES) for x in range(chips) for k in range(CORES)]
-
-    right, left, partner = pairs(1), pairs(-1), pairs(0, 1)
+        return [(x * CORES + k, (x + step * (1 - 2 * k)) % chips * CORES + (k + flip) % CORES) for x in range(chips) for k in range(CORES)]
+
+    one_way, other_way, partner = pairs(1), pairs(-1), pairs(0, 1)
 
     def send(a, where):
         return lax.ppermute(a, "dp", where)
@@ -382,13 +402,13 @@
         near, far, cuts = {0: first}, {}, {}
         for at, (i, start, size) in enumerate(parts):
             if at:
-                near[at] = send(fresh[at], right), send(fresh[at], left)
+                near[at] = send(fresh[at], one_way), send(fresh[at], other_way)
             a, b = near[at]
             by_layer = size % 2 == 0
             half = (size if by_layer else a.shape[1]) // 2
             c, d = (a[:half], b[half:]) if by_layer else (a[:, :half], b[:, half:])
             cuts[at] = (start, 0), (start + half, 0) if by_layer else (start, half)
-            far[at] = send(c, right), send(d, left)
+            far[at] = send(c, one_way), send(d, other_way)
 
         def put(at, pieces, apart=False):
             i = parts[at][0]

time: 592 us -> 586 us (0.990)
  starting transfers between devices: 31.7 us -> 21.9 us
    ppermute x30, starting transfers between devices: 31.7 us -> 21.9 us  [send(): return lax.ppermute(a, 'dp', where)]
  transfers between devices with their start and end apart: 30 -> 30, of which waited for: 10 -> 13; matrix products, arithmetic and copies ran while one was open for 6% -> 7% of each run, Pallas kernels for 8% -> 8%
where the time goes in v1:
time: 586 us
  Pallas kernels  374 us (64%)
  waiting for transfers between devices  151 us (26%)
  other arithmetic  29.7 us (5%)
  starting transfers between devices  21.9 us (4%)
  local copies, waits for them, and re-layouts  8.42 us (1%)
    pallas_call x1, Pallas kernels, reduce_and_step(): pl.pallas_call(functools.partial(reduce_kernel, chips, layers, parts), ou...  321 us
    ppermute x30, waiting for transfers between devices, send(): return lax.ppermute(a, 'dp', where)  151 us
    pallas_call x9, Pallas kernels, place(): pl.pallas_call(functools.partial(place_kernel, chips, jobs), out_shape=ja...  52.4 us
    add x3, other arithmetic, step(): new_v[w] = 0.95 * vs[w] + 0.05 * g * g  29.7 us
    ppermute x30, starting transfers between devices, send(): return lax.ppermute(a, 'dp', where)  21.9 us
  transfers between devices with their start and end apart: 30, of which 13 were waited for; matrix products, arithmetic and copies ran while one was open for 7% of the time, Pallas kernels for 8%

profile of v1, /device:TPU:113, one launch (start us, length us, event | category | flops | bytes accessed | tf_op | source)
XLA Modules:
  0.0 585.7 jit_solution(3683358437337391626)
XLA Ops:
  0.6 321.4 %reduce.1 = (bf16[2,144,4608]{2,1,0:T(8,128)(2,1)}, bf16[2,144,4608]{2,1,0:T(8,128)(2,1)}, bf16[1,576,1152]{2,1,0:T(8,128)(2,1)}, bf16[1,576,1152]{2,1,0:T(8,128...) custom-call(bf16[1,2,1152,4608]{3,2,1,0:T(8,128)(2,1)} %refs_0_.1, ...), custom_call_target="tpu_custom_call" | custom-call | tf_op jit(solution)/shard_map/reduce/pallas_call | solution.py:301
  322.0 2.4 collective-permute-start.20
  324.4 2.7 collective-permute-start.14
  327.1 1.6 slice.24
  328.6 2.8 collective-permute-start
  331.4 1.5 slice.25
  332.9 20.8 %collective-permute-done.20.refs_1_ = bf16[1,576,1152]{2,1,0:T(8,128)(2,1)S(1)} collective-permute-done((bf16[1,576,1152]{2,1,0:T(8,128)(2,1)}, bf16[1,576,1152]{2,1,0:T(8,128)(2,1)S(1)}, u32[]{:S(2)}, u32[]{:S(2)}) %collective-permute-start.20) | collective-permute-done | bytes 1327136 | tf_op jit(solution)/shard_map/ppermute | solution.py:391
  353.7 0.9 collective-permute-start.1
  354.5 2.4 collective-permute-done.22.refs_2_
  357.0 25.1 %collective-permute-done.14.refs_1_ = bf16[1,576,1152]{2,1,0:T(8,128)(2,1)S(1)} collective-permute-done((bf16[1,576,1152]{2,1,0:T(8,128)(2,1)}, bf16[1,576,1152]{2,1,0:T(8,128)(2,1)S(1)}, u32[]{:S(2)}, u32[]{:S(2)}) %collective-permute-start.14) | collective-permute-done | bytes 1327136 | tf_op jit(solution)/shard_map/ppermute | solution.py:391
  382.1 3.4 collective-permute-start.21
  385.8 24.7 %collective-permute-done.refs_0_ = bf16[1,144,4608]{2,1,0:T(8,128)(2,1)} collective-permute-done((bf16[1,144,4608]{2,1,0:T(8,128)(2,1)S(1)}, bf16[1,144,4608]{2,1,0:T(8,128)(2,1)}, u32[]{:S(2)}, u32[]{:S(2)}) %collective-permute-start) | collective-permute-done | bytes 1327136 | tf_op jit(solution)/shard_map/ppermute | solution.py:391
  410.4 3.4 collective-permute-start.15
  413.9 0.1 collective-permute-start.18
  414.0 10.7 %collective-permute-done.21.refs_0_ = bf16[1,288,1152]{2,1,0:T(8,128)(2,1)S(1)} collective-permute-done((bf16[1,288,1152]{2,1,0:T(8,128)(2,1)S(1)}, bf16[1,288,1152]{2,1,0:T(8,128)(2,1)S(1)}, u32[]{:S(2)}, u32[]{:S(2)}) %collective-permute-start.21) | collective-permute-done | bytes 663584 | tf_op jit(solution)/shard_map/ppermute | solution.py:391
  424.7 3.5 collective-permute-done.23.refs_1_
  428.2 0.1 collective-permute-start.6
  428.3 10.6 %collective-permute-done.15.refs_0_ = bf16[1,288,1152]{2,1,0:T(8,128)(2,1)} collective-permute-done((bf16[1,288,1152]{2,1,0:T(8,128)(2,1)S(1)}, bf16[1,288,1152]{2,1,0:T(8,128)(2,1)}, u32[]{:S(2)}, u32[]{:S(2)}) %collective-permute-start.15) | collective-permute-done | bytes 663584 | tf_op jit(solution)/shard_map/ppermute | solution.py:391
  439.0 2.7 collective-permute-done.18.refs_1_
  441.7 0.5 collective-permute-start.27
  442.3 2.4 collective-permute-done.26.refs_4_
  444.8 0.1 collective-permute-start.4
  444.9 1.8 collective-permute-done.27.refs_5_
  446.7 0.1 collective-permute-start.5
  446.8 0.8 collective-permute-done.24.refs_2_
  447.6 0.1 collective-permute-start.25
  447.7 8.4 %collective-permute-done.25.refs_3_ = bf16[1,288,1152]{2,1,0:T(8,128)(2,1)S(1)} collective-permute-done((bf16[1,288,1152]{2,1,0:T(8,128)(2,1)S(1)}, bf16[1,288,1152]{2,1,0:T(8,128)(2,1)S(1)}, u32[]{:S(2)}, u32[]{:S(2)}) %collective-permute-start.25) | collective-permute-done | bytes 663584 | tf_op jit(solution)/shard_map/ppermute | solution.py:391
  456.1 0.1 collective-permute-start.2
  456.3 37.0 %collective-permute-done.6.refs_1_ = bf16[2,144,4608]{2,1,0:T(8,128)(2,1)} collective-permute-done((bf16[2,144,4608]{2,1,0:T(8,128)(2,1)S(1)}, bf16[2,144,4608]{2,1,0:T(8,128)(2,1)}, u32[]{:S(2)}, u32[]{:S(2)}) %collective-permute-start.6) | collective-permute-done | bytes 2654240 | tf_op jit(solution)/shard_map/ppermute | solution.py:391
  493.3 0.5 collective-permute-start.19
  493.9 9.2 %fusion.3 = (f32[2,144,4608]{2,1,0:T(8,128)}, f32[2,144,4608]{2,1,0:T(8,128)}) fusion(bf16[2,144,4608]{2,1,0:T(8,128)(2,1)} %get-tuple-element.40, f32[2,144,4608]{2,1,0:T(8,128)} %refs_9_.1, f32[2,144,4608]{2,1,0:T(8,128)S(1)} %bitcast.1), kind=kLoop, calls=%fused_computation.9 | loop fusion | flops 10616832 | bytes 23887872 | tf_op jit(solution)/shard_map/add | solution.py:442
  503.1 2.6 slice.32
  505.7 2.5 slice.33
  508.2 2.6 collective-permute-start.7
  510.9 1.1 collective-permute-start.12
  512.0 10.1 %fusion.4 = (f32[2,144,4608]{2,1,0:T(8,128)}, f32[2,144,4608]{2,1,0:T(8,128)}) fusion(bf16[2,144,4608]{2,1,0:T(8,128)(2,1)S(1)} %copy-done.5, f32[2,144,4608]{2,1,0:T(8,128)} %refs_10_.1, f32[2,144,4608]{2,1,0:T(8,128)} %refs_7_.1), kind=kLoop, calls=%fused_computation.10 | loop fusion | flops 10616832 | bytes 23887872 | tf_op jit(solution)/shard_map/add | solution.py:442
  522.1 6.4 %place.13.refs_6_ = bf16[2,4608,1152]{2,1,0:T(8,128)(2,1)} custom-call(bf16[1,576,1152]{2,1,0:T(8,128)(2,1)} %get-tuple-element.37.refs_0_, bf16[1,576,1152]{2,1,0:T(8,128)(2,1)} %copy-done.1, bf16[1,576,1152]{2,1,0:T(8,128)(2,1)} %copy-done.3, bf16[1,576,1152]{2,1,0:T(8,128)(2,1)} %get-tuple-element.39.refs_3_, bf16[1,576,1152]{2,1,0:T(8,128)(2,1)} %copy-done.7, ...), custom_call_target="tpu_custom_call" | custom-call | flops 20000000 | bytes 15925248 | tf_op jit(solution)/shard_map/place/pallas_call | solution.py:364
  528.5 6.4 %place.14.refs_4_ = bf16[2,4608,1152]{2,1,0:T(8,128)(2,1)} custom-call(bf16[1,576,1152]{2,1,0:T(8,128)(2,1)} %get-tuple-element.36.refs_0_, bf16[1,576,1152]{2,1,0:T(8,128)(2,1)} %copy-done.2, bf16[1,576,1152]{2,1,0:T(8,128)(2,1)} %copy-done.4, bf16[1,576,1152]{2,1,0:T(8,128)(2,1)} %get-tuple-element.38.refs_3_, ...), custom_call_target="tpu_custom_call", output_to_operand_aliasing={{}: (6, {})} | custom-call | flops 20000000 | bytes 15925248 | tf_op jit(solution)/shard_map/place/pallas_call | solution.py:364
  534.9 2.7 place.15.refs_2_
  537.6 2.2 place.16.refs_2_
  539.8 2.2 place.17
  542.0 12.0 %place.9.refs_4_ = bf16[2,1152,4608]{2,1,0:T(8,128)(2,1)} custom-call(bf16[2,144,4608]{2,1,0:T(8,128)(2,1)} %get-tuple-element.30.refs_0_, bf16[2,144,4608]{2,1,0:T(8,128)(2,1)} %get-tuple-element.27.refs_1_, bf16[2,144,4608]{2,1,0:T(8,128)(2,1)} %get-tuple-element.29.refs_2_, bf16[2,144,4608]{2,1,0:T(8,128)(2,1)} %get-tuple-element.31.refs_3_, ...), custom_call_target="tpu_custom_call" | custom-call | flops 20000000 | bytes 31850496 | tf_op jit(solution)/shard_map/place/pallas_call | solution.py:364
  554.0 4.3 place.10
  558.3 0.5 collective-permute-start.10
  558.8 0.1 collective-permute-start.11
  558.9 10.5 %fusion.5 = (f32[2,576,1152]{2,1,0:T(8,128)}, f32[2,576,1152]{2,1,0:T(8,128)}) fusion(bf16[2,576,1152]{2,1,0:T(8,128)(2,1)} %get-tuple-element.42, f32[2,576,1152]{2,1,0:T(8,128)} %refs_11_.1, f32[2,576,1152]{2,1,0:T(8,128)} %refs_8_.1), kind=kLoop, calls=%fused_computation.11 | loop fusion | flops 10616832 | bytes 23887872 | tf_op jit(solution)/shard_map/add | solution.py:442
  569.4 12.0 %place.11.refs_4_ = bf16[2,1152,4608]{2,1,0:T(8,128)(2,1)} custom-call(bf16[2,144,4608]{2,1,0:T(8,128)(2,1)} %get-tuple-element.33.refs_0_, bf16[2,144,4608]{2,1,0:T(8,128)(2,1)} %collective-permute-done.6.refs_1_, bf16[2,144,4608]{2,1,0:T(8,128)(2,1)} %collective-permute-done.8.refs_2_, bf16[2,144,4608]{2,1,0:T(8,128)(2,1)} %get-tuple-element.35.refs_3_, ...), custom_call_target="tpu_custom_call" | custom-call | flops 20000000 | bytes 31850496 | tf_op jit(solution)/shard_map/place/pallas_call | solution.py:364
  581.4 4.3 place.12
  (68 shorter events, 0.7 us)
Async XLA Ops:
  322.0 171.9 %slice-start = ((s8[5308416]{0:T(1024)(128)(4,1)}), s8[4194304]{0:T(1024)(128)(4,1)S(1)}, s32[]{:S(2)}) async-start(s8[5308416]{0:T(1024)(128)(4,1)} %bitcast), calls=%async_computation | async-start | bytes 8388608
  322.0 31.6 %collective-permute-start.20 = (bf16[1,576,1152]{2,1,0:T(8,128)(2,1)}, bf16[1,576,1152]{2,1,0:T(8,128)(2,1)S(1)}, u32[]{:S(2)}, u32[]{:S(2)}) collective-permute-start(bf16[1,576,1152]{2,1,0:T(8,128)(2,1)} %get-tuple-element.37.refs_0_), channel_id=1, source_target_pairs={{0,2},{1,7},{2,4},{3,1},{4,6},{5,3},{6,0},{7,5},{8,10},{9,15},{10,... | collective-permute-start | bytes 3981320 | tf_op jit(solution)/shard_map/ppermute | solution.py:391
  324.4 32.6 %collective-permute-start.22 = (bf16[1,576,1152]{2,1,0:T(8,128)(2,1)}, bf16[1,576,1152]{2,1,0:T(8,128)(2,1)S(1)}, u32[]{:S(2)}, u32[]{:S(2)}) collective-permute-start(bf16[1,576,1152]{2,1,0:T(8,128)(2,1)} %get-tuple-element.37.refs_0_), channel_id=1, source_target_pairs={{0,6},{1,3},{2,0},{3,5},{4,2},{5,7},{6,4},{7,1},{8,14},{9,11},{10,... | collective-permute-start | bytes 3981320 | tf_op jit(solution)/shard_map/ppermute | solution.py:391
  324.4 57.7 %collective-permute-start.14 = (bf16[1,576,1152]{2,1,0:T(8,128)(2,1)}, bf16[1,576,1152]{2,1,0:T(8,128)(2,1)S(1)}, u32[]{:S(2)}, u32[]{:S(2)}) collective-permute-start(bf16[1,576,1152]{2,1,0:T(8,128)(2,1)} %get-tuple-element.36.refs_0_), channel_id=1, source_target_pairs={{0,2},{1,7},{2,4},{3,1},{4,6},{5,3},{6,0},{7,5},{8,10},{9,15},{10,... | collective-permute-start | bytes 3981320 | tf_op jit(solution)/shard_map/ppermute | solution.py:391
  327.1 58.5 %collective-permute-start.17 = (bf16[1,576,1152]{2,1,0:T(8,128)(2,1)}, bf16[1,576,1152]{2,1,0:T(8,128)(2,1)S(1)}, u32[]{:S(2)}, u32[]{:S(2)}) collective-permute-start(bf16[1,576,1152]{2,1,0:T(8,128)(2,1)} %get-tuple-element.36.refs_0_), channel_id=1, source_target_pairs={{0,6},{1,3},{2,0},{3,5},{4,2},{5,7},{6,4},{7,1},{8,14},{9,11},{10,... | collective-permute-start | bytes 3981320 | tf_op jit(solution)/shard_map/ppermute | solution.py:391
  327.1 101.1 %copy-start.6 = (bf16[2,144,4608]{2,1,0:T(8,128)(2,1)S(1)}, bf16[2,144,4608]{2,1,0:T(8,128)(2,1)}, u32[]{:S(2)}) copy-start(bf16[2,144,4608]{2,1,0:T(8,128)(2,1)} %get-tuple-element.33.refs_0_) | copy-start | bytes 7962628
  327.1 117.7 %copy-start = (bf16[2,144,4608]{2,1,0:T(8,128)(2,1)S(1)}, bf16[2,144,4608]{2,1,0:T(8,128)(2,1)}, u32[]{:S(2)}) copy-start(bf16[2,144,4608]{2,1,0:T(8,128)(2,1)} %get-tuple-element.27.refs_1_) | copy-start | bytes 7962628
  328.6 81.8 %collective-permute-start = (bf16[1,144,4608]{2,1,0:T(8,128)(2,1)S(1)}, bf16[1,144,4608]{2,1,0:T(8,128)(2,1)}, u32[]{:S(2)}, u32[]{:S(2)}) collective-permute-start(bf16[1,144,4608]{2,1,0:T(8,128)(2,1)S(1)} %slice.24), channel_id=1, source_target_pairs={{0,2},{1,7},{2,4},{3,1},{4,6},{5,3},{6,0},{7,5},{8,10},{9,15},{10,... | collective-permute-start | bytes 3981320 | tf_op jit(solution)/shard_map/ppermute | solution.py:391
  331.4 162.5 %slice-start.1 = ((s8[5308416]{0:T(1024)(128)(4,1)}), s8[1114112]{0:T(1024)(128)(4,1)S(1)}, s32[]{:S(2)}) async-start(s8[5308416]{0:T(1024)(128)(4,1)} %bitcast), calls=%async_computation.1 | async-start | bytes 2228224
  353.7 91.2 %copy-start.1 = (bf16[1,576,1152]{2,1,0:T(8,128)(2,1)}, bf16[1,576,1152]{2,1,0:T(8,128)(2,1)S(1)}, u32[]{:S(2)}) copy-start(bf16[1,576,1152]{2,1,0:T(8,128)(2,1)S(1)} %collective-permute-done.20.refs_1_) | copy-start | bytes 3981316
  353.7 60.2 %collective-permute-start.1 = (bf16[1,144,4608]{2,1,0:T(8,128)(2,1)S(1)}, bf16[1,144,4608]{2,1,0:T(8,128)(2,1)}, u32[]{:S(2)}, u32[]{:S(2)}) collective-permute-start(bf16[1,144,4608]{2,1,0:T(8,128)(2,1)S(1)} %slice.25), channel_id=1, source_target_pairs={{0,6},{1,3},{2,0},{3,5},{4,2},{5,7},{6,4},{7,1},{8,14},{9,11},{10,... | collective-permute-start | bytes 3981320 | tf_op jit(solution)/shard_map/ppermute | solution.py:391
  357.0 89.8 %copy-start.3 = (bf16[1,576,1152]{2,1,0:T(8,128)(2,1)}, bf16[1,576,1152]{2,1,0:T(8,128)(2,1)S(1)}, u32[]{:S(2)}) copy-start(bf16[1,576,1152]{2,1,0:T(8,128)(2,1)S(1)} %collective-permute-done.22.refs_2_) | copy-start | bytes 3981316
  357.0 84.7 %collective-permute-start.28 = (bf16[1,576,1152]{2,1,0:T(8,128)(2,1)S(1)}, bf16[1,576,1152]{2,1,0:T(8,128)(2,1)S(1)}, u32[]{:S(2)}, u32[]{:S(2)}) collective-permute-start(bf16[1,576,1152]{2,1,0:T(8,128)(2,1)S(1)} %collective-permute-done.20.refs_1_), channel_id=1, source_target_pairs={{0,1},{1,0},{2,3},{3,2},{4,5},{5,4},{6,7},{7,6},{8,9},{9,8},{10,11... | collective-permute-start | bytes 3981320 | tf_op jit(solution)/shard_map/ppermute | solution.py:391
  382.1 64.6 %copy-start.2 = (bf16[1,576,1152]{2,1,0:T(8,128)(2,1)}, bf16[1,576,1152]{2,1,0:T(8,128)(2,1)S(1)}, u32[]{:S(2)}) copy-start(bf16[1,576,1152]{2,1,0:T(8,128)(2,1)S(1)} %collective-permute-done.14.refs_1_) | copy-start | bytes 3981316
  382.1 42.6 %collective-permute-start.21 = (bf16[1,288,1152]{2,1,0:T(8,128)(2,1)S(1)}, bf16[1,288,1152]{2,1,0:T(8,128)(2,1)S(1)}, u32[]{:S(2)}, u32[]{:S(2)}) collective-permute-start(bf16[1,288,1152]{2,1,0:T(8,128)(2,1)S(1)} %slice.36), channel_id=1, source_target_pairs={{0,2},{1,7},{2,4},{3,1},{4,6},{5,3},{6,0},{7,5},{8,10},{9,15},{10,... | collective-permute-start | bytes 1990664 | tf_op jit(solution)/shard_map/ppermute | solution.py:391
  385.6 62.0 %copy-start.4 = (bf16[1,576,1152]{2,1,0:T(8,128)(2,1)}, bf16[1,576,1152]{2,1,0:T(8,128)(2,1)S(1)}, u32[]{:S(2)}) copy-start(bf16[1,576,1152]{2,1,0:T(8,128)(2,1)S(1)} %collective-permute-done.17.refs_2_) | copy-start | bytes 3981316
  385.6 42.6 %collective-permute-start.23 = (bf16[1,288,1152]{2,1,0:T(8,128)(2,1)S(1)}, bf16[1,288,1152]{2,1,0:T(8,128)(2,1)S(1)}, u32[]{:S(2)}, u32[]{:S(2)}) collective-permute-start(bf16[1,288,1152]{2,1,0:T(8,128)(2,1)S(1)} %slice.37), channel_id=1, source_target_pairs={{0,6},{1,3},{2,0},{3,5},{4,2},{5,7},{6,4},{7,1},{8,14},{9,11},{10,... | collective-permute-start | bytes 1990664 | tf_op jit(solution)/shard_map/ppermute | solution.py:391
  410.4 28.5 %collective-permute-start.15 = (bf16[1,288,1152]{2,1,0:T(8,128)(2,1)S(1)}, bf16[1,288,1152]{2,1,0:T(8,128)(2,1)}, u32[]{:S(2)}, u32[]{:S(2)}) collective-permute-start(bf16[1,288,1152]{2,1,0:T(8,128)(2,1)S(1)} %slice.34), channel_id=1, source_target_pairs={{0,2},{1,7},{2,4},{3,1},{4,6},{5,3},{6,0},{7,5},{8,10},{9,15},{10,... | collective-permute-start | bytes 1990664 | tf_op jit(solution)/shard_map/ppermute | solution.py:391
  413.9 27.8 %collective-permute-start.18 = (bf16[1,288,1152]{2,1,0:T(8,128)(2,1)S(1)}, bf16[1,288,1152]{2,1,0:T(8,128)(2,1)}, u32[]{:S(2)}, u32[]{:S(2)}) collective-permute-start(bf16[1,288,1152]{2,1,0:T(8,128)(2,1)S(1)} %slice.35), channel_id=1, source_target_pairs={{0,6},{1,3},{2,0},{3,5},{4,2},{5,7},{6,4},{7,1},{8,14},{9,11},{10,... | collective-permute-start | bytes 1990664 | tf_op jit(solution)/shard_map/ppermute | solution.py:391
  424.7 69.2 %copy-start.11 = (bf16[1,288,1152]{2,1,0:T(8,128)(2,1)}, bf16[1,288,1152]{2,1,0:T(8,128)(2,1)S(1)}, u32[]{:S(2)}) copy-start(bf16[1,288,1152]{2,1,0:T(8,128)(2,1)S(1)} %collective-permute-done.21.refs_0_) | copy-start | bytes 1990660
  424.7 17.5 %collective-permute-start.29 = (bf16[1,576,1152]{2,1,0:T(8,128)(2,1)S(1)}, bf16[1,576,1152]{2,1,0:T(8,128)(2,1)S(1)}, u32[]{:S(2)}, u32[]{:S(2)}) collective-permute-start(bf16[1,576,1152]{2,1,0:T(8,128)(2,1)S(1)} %collective-permute-done.22.refs_2_), channel_id=1, source_target_pairs={{0,1},{1,0},{2,3},{3,2},{4,5},{5,4},{6,7},{7,6},{8,9},{9,8},{10,11... | collective-permute-start | bytes 3981320 | tf_op jit(solution)/shard_map/ppermute | solution.py:391
  428.2 65.7 %copy-start.12 = (bf16[1,288,1152]{2,1,0:T(8,128)(2,1)}, bf16[1,288,1152]{2,1,0:T(8,128)(2,1)S(1)}, u32[]{:S(2)}) copy-start(bf16[1,288,1152]{2,1,0:T(8,128)(2,1)S(1)} %collective-permute-done.23.refs_1_) | copy-start | bytes 1990660
  428.2 65.1 %collective-permute-start.6 = (bf16[2,144,4608]{2,1,0:T(8,128)(2,1)S(1)}, bf16[2,144,4608]{2,1,0:T(8,128)(2,1)}, u32[]{:S(2)}, u32[]{:S(2)}) collective-permute-start(bf16[2,144,4608]{2,1,0:T(8,128)(2,1)S(1)} %copy-done.6), channel_id=1, source_target_pairs={{0,2},{1,7},{2,4},{3,1},{4,6},{5,3},{6,0},{7,5},{8,10},{9,15},{10,... | collective-permute-start | bytes 7962632 | tf_op jit(solution)/shard_map/ppermute | solution.py:391
  438.9 54.4 %collective-permute-start.8 = (bf16[2,144,4608]{2,1,0:T(8,128)(2,1)S(1)}, bf16[2,144,4608]{2,1,0:T(8,128)(2,1)}, u32[]{:S(2)}, u32[]{:S(2)}) collective-permute-start(bf16[2,144,4608]{2,1,0:T(8,128)(2,1)S(1)} %copy-done.6), channel_id=1, source_target_pairs={{0,6},{1,3},{2,0},{3,5},{4,2},{5,7},{6,4},{7,1},{8,14},{9,11},{10,... | collective-permute-start | bytes 7962632 | tf_op jit(solution)/shard_map/ppermute | solution.py:391
  441.7 3.1 collective-permute-start.26
  441.7 51.6 %copy-start.7 = (bf16[1,576,1152]{2,1,0:T(8,128)(2,1)}, bf16[1,576,1152]{2,1,0:T(8,128)(2,1)S(1)}, u32[]{:S(2)}) copy-start(bf16[1,576,1152]{2,1,0:T(8,128)(2,1)S(1)} %collective-permute-done.28.refs_4_) | copy-start | bytes 3981316
  441.7 4.9 collective-permute-start.27
  442.2 51.6 %copy-start.8 = (bf16[1,576,1152]{2,1,0:T(8,128)(2,1)}, bf16[1,576,1152]{2,1,0:T(8,128)(2,1)S(1)}, u32[]{:S(2)}) copy-start(bf16[1,576,1152]{2,1,0:T(8,128)(2,1)S(1)} %collective-permute-done.29.refs_5_) | copy-start | bytes 3981316
  442.2 5.4 collective-permute-start.24
  444.8 49.1 %copy-start.9 = (bf16[1,576,1152]{2,1,0:T(8,128)(2,1)}, bf16[1,576,1152]{2,1,0:T(8,128)(2,1)S(1)}, u32[]{:S(2)}) copy-start(bf16[1,576,1152]{2,1,0:T(8,128)(2,1)S(1)} %collective-permute-done.26.refs_4_) | copy-start | bytes 3981316
  444.8 66.1 %collective-permute-start.4 = (bf16[2,144,4608]{2,1,0:T(8,128)(2,1)S(1)}, bf16[2,144,4608]{2,1,0:T(8,128)(2,1)}, u32[]{:S(2)}, u32[]{:S(2)}) collective-permute-start(bf16[2,144,4608]{2,1,0:T(8,128)(2,1)S(1)} %copy-done), channel_id=1, source_target_pairs={{0,1},{1,0},{2,3},{3,2},{4,5},{5,4},{6,7},{7,6},{8,9},{9,8},{10,11... | collective-permute-start | bytes 7962632 | tf_op jit(solution)/shard_map/ppermute | solution.py:391
  446.7 47.2 %copy-start.10 = (bf16[1,576,1152]{2,1,0:T(8,128)(2,1)}, bf16[1,576,1152]{2,1,0:T(8,128)(2,1)S(1)}, u32[]{:S(2)}) copy-start(bf16[1,576,1152]{2,1,0:T(8,128)(2,1)S(1)} %collective-permute-done.27.refs_5_) | copy-start | bytes 3981316
  446.7 64.2 %collective-permute-start.5 = (bf16[2,144,4608]{2,1,0:T(8,128)(2,1)}, bf16[2,144,4608]{2,1,0:T(8,128)(2,1)}, u32[]{:S(2)}, u32[]{:S(2)}) collective-permute-start(bf16[2,144,4608]{2,1,0:T(8,128)(2,1)} %get-tuple-element.29.refs_2_), channel_id=1, source_target_pairs={{0,1},{1,0},{2,3},{3,2},{4,5},{5,4},{6,7},{7,6},{8,9},{9,8},{10,11... | collective-permute-start | bytes 7962632 | tf_op jit(solution)/shard_map/ppermute | solution.py:391
  447.6 46.3 %copy-start.13 = (bf16[1,288,1152]{2,1,0:T(8,128)(2,1)}, bf16[1,288,1152]{2,1,0:T(8,128)(2,1)S(1)}, u32[]{:S(2)}) copy-start(bf16[1,288,1152]{2,1,0:T(8,128)(2,1)S(1)} %collective-permute-done.24.refs_2_) | copy-start | bytes 1990660
  447.6 8.5 %collective-permute-start.25 = (bf16[1,288,1152]{2,1,0:T(8,128)(2,1)S(1)}, bf16[1,288,1152]{2,1,0:T(8,128)(2,1)S(1)}, u32[]{:S(2)}, u32[]{:S(2)}) collective-permute-start(bf16[1,288,1152]{2,1,0:T(8,128)(2,1)S(1)} %collective-permute-done.23.refs_1_), channel_id=1, source_target_pairs={{0,1},{1,0},{2,3},{3,2},{4,5},{5,4},{6,7},{7,6},{8,9},{9,8},{10,11... | collective-permute-start | bytes 1990664 | tf_op jit(solution)/shard_map/ppermute | solution.py:391
  456.1 37.7 %copy-start.14 = (bf16[1,288,1152]{2,1,0:T(8,128)(2,1)}, bf16[1,288,1152]{2,1,0:T(8,128)(2,1)S(1)}, u32[]{:S(2)}) copy-start(bf16[1,288,1152]{2,1,0:T(8,128)(2,1)S(1)} %collective-permute-done.25.refs_3_) | copy-start | bytes 1990660
  456.1 55.8 %collective-permute-start.2 = (bf16[1,144,4608]{2,1,0:T(8,128)(2,1)}, bf16[1,144,4608]{2,1,0:T(8,128)(2,1)}, u32[]{:S(2)}, u32[]{:S(2)}) collective-permute-start(bf16[1,144,4608]{2,1,0:T(8,128)(2,1)} %collective-permute-done.refs_0_), channel_id=1, source_target_pairs={{0,1},{1,0},{2,3},{3,2},{4,5},{5,4},{6,7},{7,6},{8,9},{9,8},{10,11... | collective-permute-start | bytes 3981320 | tf_op jit(solution)/shard_map/ppermute | solution.py:391
  493.3 14.8 %collective-permute-start.16 = (bf16[1,288,1152]{2,1,0:T(8,128)(2,1)}, bf16[1,288,1152]{2,1,0:T(8,128)(2,1)}, u32[]{:S(2)}, u32[]{:S(2)}) collective-permute-start(bf16[1,288,1152]{2,1,0:T(8,128)(2,1)} %collective-permute-done.15.refs_0_), channel_id=1, source_target_pairs={{0,1},{1,0},{2,3},{3,2},{4,5},{5,4},{6,7},{7,6},{8,9},{9,8},{10,11... | collective-permute-start | bytes 1990664 | tf_op jit(solution)/shard_map/ppermute | solution.py:391
  493.3 14.9 %collective-permute-start.19 = (bf16[1,288,1152]{2,1,0:T(8,128)(2,1)}, bf16[1,288,1152]{2,1,0:T(8,128)(2,1)}, u32[]{:S(2)}, u32[]{:S(2)}) collective-permute-start(bf16[1,288,1152]{2,1,0:T(8,128)(2,1)} %collective-permute-done.18.refs_1_), channel_id=1, source_target_pairs={{0,1},{1,0},{2,3},{3,2},{4,5},{5,4},{6,7},{7,6},{8,9},{9,8},{10,11... | collective-permute-start | bytes 1990664 | tf_op jit(solution)/shard_map/ppermute | solution.py:391
  503.1 8.9 %copy-start.5 = (bf16[2,144,4608]{2,1,0:T(8,128)(2,1)S(1)}, bf16[2,144,4608]{2,1,0:T(8,128)(2,1)}, u32[]{:S(2)}) copy-start(bf16[2,144,4608]{2,1,0:T(8,128)(2,1)} %get-tuple-element.41) | copy-start | bytes 7962628
  508.2 45.8 %collective-permute-start.3 = (bf16[1,144,4608]{2,1,0:T(8,128)(2,1)}, bf16[1,144,4608]{2,1,0:T(8,128)(2,1)}, u32[]{:S(2)}, u32[]{:S(2)}) collective-permute-start(bf16[1,144,4608]{2,1,0:T(8,128)(2,1)} %collective-permute-done.1.refs_1_), channel_id=1, source_target_pairs={{0,1},{1,0},{2,3},{3,2},{4,5},{5,4},{6,7},{7,6},{8,9},{9,8},{10,11... | collective-permute-start | bytes 3981320 | tf_op jit(solution)/shard_map/ppermute | solution.py:391
  508.2 50.1 %collective-permute-start.7 = (bf16[1,144,4608]{2,1,0:T(8,128)(2,1)}, bf16[1,144,4608]{2,1,0:T(8,128)(2,1)}, u32[]{:S(2)}, u32[]{:S(2)}) collective-permute-start(bf16[1,144,4608]{2,1,0:T(8,128)(2,1)} %slice.32), channel_id=1, source_target_pairs={{0,2},{1,7},{2,4},{3,1},{4,6},{5,3},{6,0},{7,5},{8,10},{9,15},{10,... | collective-permute-start | bytes 3981320 | tf_op jit(solution)/shard_map/ppermute | solution.py:391
  510.9 48.0 %collective-permute-start.9 = (bf16[1,144,4608]{2,1,0:T(8,128)(2,1)}, bf16[1,144,4608]{2,1,0:T(8,128)(2,1)}, u32[]{:S(2)}, u32[]{:S(2)}) collective-permute-start(bf16[1,144,4608]{2,1,0:T(8,128)(2,1)} %slice.33), channel_id=1, source_target_pairs={{0,6},{1,3},{2,0},{3,5},{4,2},{5,7},{6,4},{7,1},{8,14},{9,11},{10,... | collective-permute-start | bytes 3981320 | tf_op jit(solution)/shard_map/ppermute | solution.py:391
  510.9 58.5 %collective-permute-start.12 = (bf16[2,144,4608]{2,1,0:T(8,128)(2,1)}, bf16[2,144,4608]{2,1,0:T(8,128)(2,1)}, u32[]{:S(2)}, u32[]{:S(2)}) collective-permute-start(bf16[2,144,4608]{2,1,0:T(8,128)(2,1)} %collective-permute-done.6.refs_1_), channel_id=1, source_target_pairs={{0,1},{1,0},{2,3},{3,2},{4,5},{5,4},{6,7},{7,6},{8,9},{9,8},{10,11... | collective-permute-start | bytes 7962632 | tf_op jit(solution)/shard_map/ppermute | solution.py:391
  511.9 57.5 %collective-permute-start.13 = (bf16[2,144,4608]{2,1,0:T(8,128)(2,1)}, bf16[2,144,4608]{2,1,0:T(8,128)(2,1)}, u32[]{:S(2)}, u32[]{:S(2)}) collective-permute-start(bf16[2,144,4608]{2,1,0:T(8,128)(2,1)} %collective-permute-done.8.refs_2_), channel_id=1, source_target_pairs={{0,1},{1,0},{2,3},{3,2},{4,5},{5,4},{6,7},{7,6},{8,9},{9,8},{10,11... | collective-permute-start | bytes 7962632 | tf_op jit(solution)/shard_map/ppermute | solution.py:391
  558.3 23.1 %collective-permute-start.10 = (bf16[1,144,4608]{2,1,0:T(8,128)(2,1)}, bf16[1,144,4608]{2,1,0:T(8,128)(2,1)}, u32[]{:S(2)}, u32[]{:S(2)}) collective-permute-start(bf16[1,144,4608]{2,1,0:T(8,128)(2,1)} %collective-permute-done.7.refs_0_), channel_id=1, source_target_pairs={{0,1},{1,0},{2,3},{3,2},{4,5},{5,4},{6,7},{7,6},{8,9},{9,8},{10,11... | collective-permute-start | bytes 3981320 | tf_op jit(solution)/shard_map/ppermute | solution.py:391
  558.8 22.6 %collective-permute-start.11 = (bf16[1,144,4608]{2,1,0:T(8,128)(2,1)}, bf16[1,144,4608]{2,1,0:T(8,128)(2,1)}, u32[]{:S(2)}, u32[]{:S(2)}) collective-permute-start(bf16[1,144,4608]{2,1,0:T(8,128)(2,1)} %collective-permute-done.9.refs_1_), channel_id=1, source_target_pairs={{0,1},{1,0},{2,3},{3,2},{4,5},{5,4},{6,7},{7,6},{8,9},{9,8},{10,11... | collective-permute-start | bytes 3981320 | tf_op jit(solution)/shard_map/ppermute | solution.py:391

commit v2 on v1

--- a/solution.py
+++ b/solution.py
@@ -13,6 +13,7 @@
 STRIP = 16
 SLOTS = 4
 GROUPS = 3
+EARLY = (2, 3)
 MESH = pl.DeviceIdType.MESH
 ORDER = (2, 1, 3, 0)
 
@@ -430,12 +431,15 @@
             (c, d), ((c_layer, c_row), (d_layer, d_row)) = far[at], cuts[at]
             put(at, [(c, None, c_layer, 2, c_row), (d, None, d_layer, 2, d_row)], apart)
 
+        for at in EARLY:
+            put(at, [(fresh[at], other[at], parts[at][1], 0, 0)])
         for at, (i, start, _) in enumerate(parts):
             a, b = near[at]
-            put(at, [(fresh[at], other[at], start, 0, 0), (a, None, start, chips - 1, 0), (b, None, start, 1, 0)])
+            home = [] if at in EARLY else [(fresh[at], other[at], start, 0, 0)]
+            put(at, home + [(a, None, start, chips - 1, 0), (b, None, start, 1, 0)], at == last)
             if at:
-                put_far(at - 1)
-        put_far(last, apart=True)
+                put_far(at - 1, at == last)
+        put_far(last, True)
         for w in range(3):
             g = gradients[w].astype(f32)
             new_m[w] = 0.9 * ms[w] + 0.1 * g

time: 586 us -> 590 us (level)
    pallas_call x9 -> x13, Pallas kernels: 52.4 us -> 57.1 us  [place(): pl.pallas_call(functools.partial(place_kernel, chips, jobs), out_shape=ja...]
  transfers between devices with their start and end apart: 30 -> 30, of which waited for: 13 -> 13; matrix products, arithmetic and copies ran while one was open for 7% -> 6% of each run, Pallas kernels for 8% -> 9%
where the time goes in v2:
time: 590 us
  Pallas kernels  378 us (64%)
  waiting for transfers between devices  151 us (26%)
  other arithmetic  28.9 us (5%)
  starting transfers between devices  22 us (4%)
  local copies, waits for them, and re-layouts  8.42 us (1%)
    pallas_call x1, Pallas kernels, reduce_and_step(): pl.pallas_call(functools.partial(reduce_kernel, chips, layers, parts), ou...  321 us
    ppermute x30, waiting for transfers between devices, send(): return lax.ppermute(a, 'dp', where)  151 us
    pallas_call x13, Pallas kernels, place(): pl.pallas_call(functools.partial(place_kernel, chips, jobs), out_shape=ja...  57.1 us
    add x3, other arithmetic, step(): new_v[w] = 0.95 * vs[w] + 0.05 * g * g  28.9 us
    ppermute x30, starting transfers between devices, send(): return lax.ppermute(a, 'dp', where)  22 us
  transfers between devices with their start and end apart: 30, of which 13 were waited for; matrix products, arithmetic and copies ran while one was open for 6% of the time, Pallas kernels for 9%

profile of v2, /device:TPU:113, one launch (start us, length us, event | category | flops | bytes accessed | tf_op | source)
XLA Modules:
  0.0 589.6 jit_solution(1796026836043900787)
XLA Ops:
  0.6 321.4 %reduce.1 = (bf16[2,144,4608]{2,1,0:T(8,128)(2,1)}, bf16[2,144,4608]{2,1,0:T(8,128)(2,1)}, bf16[1,576,1152]{2,1,0:T(8,128)(2,1)}, bf16[1,576,1152]{2,1,0:T(8,128...) custom-call(bf16[1,2,1152,4608]{3,2,1,0:T(8,128)(2,1)} %refs_0_.1, ...), custom_call_target="tpu_custom_call" | custom-call | tf_op jit(solution)/shard_map/reduce/pallas_call | solution.py:302
  322.0 2.4 collective-permute-start.20
  324.4 2.7 collective-permute-start.14
  327.1 1.6 slice.24
  328.6 2.8 collective-permute-start
  331.4 1.5 slice.25
  332.9 20.8 %collective-permute-done.20.refs_0_ = bf16[1,576,1152]{2,1,0:T(8,128)(2,1)S(1)} collective-permute-done((bf16[1,576,1152]{2,1,0:T(8,128)(2,1)}, bf16[1,576,1152]{2,1,0:T(8,128)(2,1)S(1)}, u32[]{:S(2)}, u32[]{:S(2)}) %collective-permute-start.20) | collective-permute-done | bytes 1327136 | tf_op jit(solution)/shard_map/ppermute | solution.py:392
  353.7 0.9 collective-permute-start.1
  354.5 2.4 collective-permute-done.23.refs_1_
  357.0 25.1 %collective-permute-done.14.refs_0_ = bf16[1,576,1152]{2,1,0:T(8,128)(2,1)S(1)} collective-permute-done((bf16[1,576,1152]{2,1,0:T(8,128)(2,1)}, bf16[1,576,1152]{2,1,0:T(8,128)(2,1)S(1)}, u32[]{:S(2)}, u32[]{:S(2)}) %collective-permute-start.14) | collective-permute-done | bytes 1327136 | tf_op jit(solution)/shard_map/ppermute | solution.py:392
  382.1 3.4 collective-permute-start.21
  385.8 24.7 %collective-permute-done.refs_0_ = bf16[1,144,4608]{2,1,0:T(8,128)(2,1)} collective-permute-done((bf16[1,144,4608]{2,1,0:T(8,128)(2,1)S(1)}, bf16[1,144,4608]{2,1,0:T(8,128)(2,1)}, u32[]{:S(2)}, u32[]{:S(2)}) %collective-permute-start) | collective-permute-done | bytes 1327136 | tf_op jit(solution)/shard_map/ppermute | solution.py:392
  410.4 3.4 collective-permute-start.15
  414.0 10.7 %collective-permute-done.21.refs_0_ = bf16[1,288,1152]{2,1,0:T(8,128)(2,1)S(1)} collective-permute-done((bf16[1,288,1152]{2,1,0:T(8,128)(2,1)S(1)}, bf16[1,288,1152]{2,1,0:T(8,128)(2,1)S(1)}, u32[]{:S(2)}, u32[]{:S(2)}) %collective-permute-start.21) | collective-permute-done | bytes 663584 | tf_op jit(solution)/shard_map/ppermute | solution.py:392
  424.7 3.5 collective-permute-done.24.refs_1_
  428.3 10.6 %collective-permute-done.15.refs_0_ = bf16[1,288,1152]{2,1,0:T(8,128)(2,1)} collective-permute-done((bf16[1,288,1152]{2,1,0:T(8,128)(2,1)S(1)}, bf16[1,288,1152]{2,1,0:T(8,128)(2,1)}, u32[]{:S(2)}, u32[]{:S(2)}) %collective-permute-start.15) | collective-permute-done | bytes 663584 | tf_op jit(solution)/shard_map/ppermute | solution.py:392
  439.0 2.7 collective-permute-done.18.refs_1_
  441.7 0.6 collective-permute-start.27
  442.4 2.4 collective-permute-done.26.refs_0_
  444.8 0.1 collective-permute-start.4
  444.9 1.8 collective-permute-done.27.refs_1_
  446.7 0.1 collective-permute-start.5
  446.8 0.8 collective-permute-done.22.refs_0_
  447.6 0.1 collective-permute-start.25
  447.7 8.4 %collective-permute-done.25.refs_1_ = bf16[1,288,1152]{2,1,0:T(8,128)(2,1)S(1)} collective-permute-done((bf16[1,288,1152]{2,1,0:T(8,128)(2,1)S(1)}, bf16[1,288,1152]{2,1,0:T(8,128)(2,1)S(1)}, u32[]{:S(2)}, u32[]{:S(2)}) %collective-permute-start.25) | collective-permute-done | bytes 663584 | tf_op jit(solution)/shard_map/ppermute | solution.py:392
  456.3 37.0 %collective-permute-done.6.refs_1_ = bf16[2,144,4608]{2,1,0:T(8,128)(2,1)} collective-permute-done((bf16[2,144,4608]{2,1,0:T(8,128)(2,1)S(1)}, bf16[2,144,4608]{2,1,0:T(8,128)(2,1)}, u32[]{:S(2)}, u32[]{:S(2)}) %collective-permute-start.6) | collective-permute-done | bytes 2654240 | tf_op jit(solution)/shard_map/ppermute | solution.py:392
  493.3 0.5 collective-permute-start.19
  493.9 8.3 %fusion.3 = (f32[2,144,4608]{2,1,0:T(8,128)}, f32[2,144,4608]{2,1,0:T(8,128)}) fusion(bf16[2,144,4608]{2,1,0:T(8,128)(2,1)S(1)} %copy-done.5, f32[2,144,4608]{2,1,0:T(8,128)} %refs_9_.1, f32[2,144,4608]{2,1,0:T(8,128)S(1)} %bitcast.1), kind=kLoop, calls=%fused_computation.9 | loop fusion | flops 10616832 | bytes 23887872 | tf_op jit(solution)/shard_map/add | solution.py:446
  502.3 2.9 place.17.refs_2_
  505.1 2.9 place.18.refs_4_
  508.0 2.6 slice.32
  510.6 2.5 slice.33
  513.2 2.6 collective-permute-start.7
  515.8 1.1 collective-permute-start.12
  516.9 10.1 %fusion.4 = (f32[2,144,4608]{2,1,0:T(8,128)}, f32[2,144,4608]{2,1,0:T(8,128)}) fusion(bf16[2,144,4608]{2,1,0:T(8,128)(2,1)S(1)} %copy-done.4, f32[2,144,4608]{2,1,0:T(8,128)} %refs_10_.1, f32[2,144,4608]{2,1,0:T(8,128)} %refs_7_.1), kind=kLoop, calls=%fused_computation.10 | loop fusion | flops 10616832 | bytes 23887872 | tf_op jit(solution)/shard_map/add | solution.py:446
  527.1 4.3 place.19.refs_2_
  531.4 2.9 place.20.refs_2_
  534.2 2.9 place.21.refs_2_
  537.1 2.2 place.22.refs_2_
  539.3 2.2 place.23.refs_2_
  541.5 2.2 place.24.refs_2_
  543.7 2.2 place.25
  545.9 12.0 %place.13.refs_4_ = bf16[2,1152,4608]{2,1,0:T(8,128)(2,1)} custom-call(bf16[2,144,4608]{2,1,0:T(8,128)(2,1)} %get-tuple-element.30.refs_0_, bf16[2,144,4608]{2,1,0:T(8,128)(2,1)} %get-tuple-element.27.refs_1_, bf16[2,144,4608]{2,1,0:T(8,128)(2,1)} %get-tuple-element.29.refs_2_, bf16[2,144,4608]{2,1,0:T(8,128)(2,1)} %get-tuple-element.31.refs_3_, ...), custom_call_target="tpu_custom_call" | custom-call | flops 20000000 | bytes 31850496 | tf_op jit(solution)/shard_map/place/pallas_call | solution.py:365
  557.9 4.3 place.14
  562.2 0.5 collective-permute-start.10
  562.8 10.5 %fusion.5 = (f32[2,576,1152]{2,1,0:T(8,128)}, f32[2,576,1152]{2,1,0:T(8,128)}) fusion(bf16[2,576,1152]{2,1,0:T(8,128)(2,1)} %get-tuple-element.42, f32[2,576,1152]{2,1,0:T(8,128)} %refs_11_.1, f32[2,576,1152]{2,1,0:T(8,128)} %refs_8_.1), kind=kLoop, calls=%fused_computation.11 | loop fusion | flops 10616832 | bytes 23887872 | tf_op jit(solution)/shard_map/add | solution.py:446
  573.3 12.0 %place.15.refs_4_ = bf16[2,1152,4608]{2,1,0:T(8,128)(2,1)} custom-call(bf16[2,144,4608]{2,1,0:T(8,128)(2,1)} %get-tuple-element.33.refs_0_, bf16[2,144,4608]{2,1,0:T(8,128)(2,1)} %collective-permute-done.6.refs_1_, bf16[2,144,4608]{2,1,0:T(8,128)(2,1)} %collective-permute-done.8.refs_2_, bf16[2,144,4608]{2,1,0:T(8,128)(2,1)} %get-tuple-element.35.refs_3_, ...), custom_call_target="tpu_custom_call" | custom-call | flops 20000000 | bytes 31850496 | tf_op jit(solution)/shard_map/place/pallas_call | solution.py:365
  585.3 4.3 place.16
  (72 shorter events, 1.2 us)
Async XLA Ops:
  322.0 171.9 %slice-start = ((s8[5308416]{0:T(1024)(128)(4,1)}), s8[4194304]{0:T(1024)(128)(4,1)S(1)}, s32[]{:S(2)}) async-start(s8[5308416]{0:T(1024)(128)(4,1)} %bitcast), calls=%async_computation | async-start | bytes 8388608
  322.0 31.6 %collective-permute-start.20 = (bf16[1,576,1152]{2,1,0:T(8,128)(2,1)}, bf16[1,576,1152]{2,1,0:T(8,128)(2,1)S(1)}, u32[]{:S(2)}, u32[]{:S(2)}) collective-permute-start(bf16[1,576,1152]{2,1,0:T(8,128)(2,1)} %get-tuple-element.37.refs_0_), channel_id=1, source_target_pairs={{0,2},{1,7},{2,4},{3,1},{4,6},{5,3},{6,0},{7,5},{8,10},{9,15},{10,... | collective-permute-start | bytes 3981320 | tf_op jit(solution)/shard_map/ppermute | solution.py:392
  324.4 32.6 %collective-permute-start.23 = (bf16[1,576,1152]{2,1,0:T(8,128)(2,1)}, bf16[1,576,1152]{2,1,0:T(8,128)(2,1)S(1)}, u32[]{:S(2)}, u32[]{:S(2)}) collective-permute-start(bf16[1,576,1152]{2,1,0:T(8,128)(2,1)} %get-tuple-element.37.refs_0_), channel_id=1, source_target_pairs={{0,6},{1,3},{2,0},{3,5},{4,2},{5,7},{6,4},{7,1},{8,14},{9,11},{10,... | collective-permute-start | bytes 3981320 | tf_op jit(solution)/shard_map/ppermute | solution.py:392
  324.4 57.7 %collective-permute-start.14 = (bf16[1,576,1152]{2,1,0:T(8,128)(2,1)}, bf16[1,576,1152]{2,1,0:T(8,128)(2,1)S(1)}, u32[]{:S(2)}, u32[]{:S(2)}) collective-permute-start(bf16[1,576,1152]{2,1,0:T(8,128)(2,1)} %get-tuple-element.36.refs_0_), channel_id=1, source_target_pairs={{0,2},{1,7},{2,4},{3,1},{4,6},{5,3},{6,0},{7,5},{8,10},{9,15},{10,... | collective-permute-start | bytes 3981320 | tf_op jit(solution)/shard_map/ppermute | solution.py:392
  327.1 58.5 %collective-permute-start.17 = (bf16[1,576,1152]{2,1,0:T(8,128)(2,1)}, bf16[1,576,1152]{2,1,0:T(8,128)(2,1)S(1)}, u32[]{:S(2)}, u32[]{:S(2)}) collective-permute-start(bf16[1,576,1152]{2,1,0:T(8,128)(2,1)} %get-tuple-element.36.refs_0_), channel_id=1, source_target_pairs={{0,6},{1,3},{2,0},{3,5},{4,2},{5,7},{6,4},{7,1},{8,14},{9,11},{10,... | collective-permute-start | bytes 3981320 | tf_op jit(solution)/shard_map/ppermute | solution.py:392
  327.1 101.1 %copy-start.6 = (bf16[2,144,4608]{2,1,0:T(8,128)(2,1)S(1)}, bf16[2,144,4608]{2,1,0:T(8,128)(2,1)}, u32[]{:S(2)}) copy-start(bf16[2,144,4608]{2,1,0:T(8,128)(2,1)} %get-tuple-element.33.refs_0_) | copy-start | bytes 7962628
  327.1 166.8 %copy-start.5 = (bf16[2,144,4608]{2,1,0:T(8,128)(2,1)S(1)}, bf16[2,144,4608]{2,1,0:T(8,128)(2,1)}, u32[]{:S(2)}) copy-start(bf16[2,144,4608]{2,1,0:T(8,128)(2,1)} %get-tuple-element.40) | copy-start | bytes 7962628
  328.6 81.8 %collective-permute-start = (bf16[1,144,4608]{2,1,0:T(8,128)(2,1)S(1)}, bf16[1,144,4608]{2,1,0:T(8,128)(2,1)}, u32[]{:S(2)}, u32[]{:S(2)}) collective-permute-start(bf16[1,144,4608]{2,1,0:T(8,128)(2,1)S(1)} %slice.24), channel_id=1, source_target_pairs={{0,2},{1,7},{2,4},{3,1},{4,6},{5,3},{6,0},{7,5},{8,10},{9,15},{10,... | collective-permute-start | bytes 3981320 | tf_op jit(solution)/shard_map/ppermute | solution.py:392
  331.4 162.5 %slice-start.1 = ((s8[5308416]{0:T(1024)(128)(4,1)}), s8[1114112]{0:T(1024)(128)(4,1)S(1)}, s32[]{:S(2)}) async-start(s8[5308416]{0:T(1024)(128)(4,1)} %bitcast), calls=%async_computation.1 | async-start | bytes 2228224
  353.7 3.3 copy-start
  353.7 60.2 %collective-permute-start.1 = (bf16[1,144,4608]{2,1,0:T(8,128)(2,1)S(1)}, bf16[1,144,4608]{2,1,0:T(8,128)(2,1)}, u32[]{:S(2)}, u32[]{:S(2)}) collective-permute-start(bf16[1,144,4608]{2,1,0:T(8,128)(2,1)S(1)} %slice.25), channel_id=1, source_target_pairs={{0,6},{1,3},{2,0},{3,5},{4,2},{5,7},{6,4},{7,1},{8,14},{9,11},{10,... | collective-permute-start | bytes 3981320 | tf_op jit(solution)/shard_map/ppermute | solution.py:392
  357.0 87.8 %copy-start.2 = (bf16[1,576,1152]{2,1,0:T(8,128)(2,1)}, bf16[1,576,1152]{2,1,0:T(8,128)(2,1)S(1)}, u32[]{:S(2)}) copy-start(bf16[1,576,1152]{2,1,0:T(8,128)(2,1)S(1)} %collective-permute-done.23.refs_1_) | copy-start | bytes 3981316
  357.0 84.7 %collective-permute-start.28 = (bf16[1,576,1152]{2,1,0:T(8,128)(2,1)S(1)}, bf16[1,576,1152]{2,1,0:T(8,128)(2,1)S(1)}, u32[]{:S(2)}, u32[]{:S(2)}) collective-permute-start(bf16[1,576,1152]{2,1,0:T(8,128)(2,1)S(1)} %collective-permute-done.20.refs_0_), channel_id=1, source_target_pairs={{0,1},{1,0},{2,3},{3,2},{4,5},{5,4},{6,7},{7,6},{8,9},{9,8},{10,11... | collective-permute-start | bytes 3981320 | tf_op jit(solution)/shard_map/ppermute | solution.py:392
  382.1 59.6 %copy-start.1 = (bf16[1,576,1152]{2,1,0:T(8,128)(2,1)}, bf16[1,576,1152]{2,1,0:T(8,128)(2,1)S(1)}, u32[]{:S(2)}) copy-start(bf16[1,576,1152]{2,1,0:T(8,128)(2,1)S(1)} %collective-permute-done.14.refs_0_) | copy-start | bytes 3981316
  382.1 42.6 %collective-permute-start.21 = (bf16[1,288,1152]{2,1,0:T(8,128)(2,1)S(1)}, bf16[1,288,1152]{2,1,0:T(8,128)(2,1)S(1)}, u32[]{:S(2)}, u32[]{:S(2)}) collective-permute-start(bf16[1,288,1152]{2,1,0:T(8,128)(2,1)S(1)} %slice.36), channel_id=1, source_target_pairs={{0,2},{1,7},{2,4},{3,1},{4,6},{5,3},{6,0},{7,5},{8,10},{9,15},{10,... | collective-permute-start | bytes 1990664 | tf_op jit(solution)/shard_map/ppermute | solution.py:392
  385.6 59.3 %copy-start.3 = (bf16[1,576,1152]{2,1,0:T(8,128)(2,1)}, bf16[1,576,1152]{2,1,0:T(8,128)(2,1)S(1)}, u32[]{:S(2)}) copy-start(bf16[1,576,1152]{2,1,0:T(8,128)(2,1)S(1)} %collective-permute-done.17.refs_1_) | copy-start | bytes 3981316
  385.6 42.6 %collective-permute-start.24 = (bf16[1,288,1152]{2,1,0:T(8,128)(2,1)S(1)}, bf16[1,288,1152]{2,1,0:T(8,128)(2,1)S(1)}, u32[]{:S(2)}, u32[]{:S(2)}) collective-permute-start(bf16[1,288,1152]{2,1,0:T(8,128)(2,1)S(1)} %slice.37), channel_id=1, source_target_pairs={{0,6},{1,3},{2,0},{3,5},{4,2},{5,7},{6,4},{7,1},{8,14},{9,11},{10,... | collective-permute-start | bytes 1990664 | tf_op jit(solution)/shard_map/ppermute | solution.py:392
  410.4 28.5 %collective-permute-start.15 = (bf16[1,288,1152]{2,1,0:T(8,128)(2,1)S(1)}, bf16[1,288,1152]{2,1,0:T(8,128)(2,1)}, u32[]{:S(2)}, u32[]{:S(2)}) collective-permute-start(bf16[1,288,1152]{2,1,0:T(8,128)(2,1)S(1)} %slice.34), channel_id=1, source_target_pairs={{0,2},{1,7},{2,4},{3,1},{4,6},{5,3},{6,0},{7,5},{8,10},{9,15},{10,... | collective-permute-start | bytes 1990664 | tf_op jit(solution)/shard_map/ppermute | solution.py:392
  413.9 27.8 %collective-permute-start.18 = (bf16[1,288,1152]{2,1,0:T(8,128)(2,1)S(1)}, bf16[1,288,1152]{2,1,0:T(8,128)(2,1)}, u32[]{:S(2)}, u32[]{:S(2)}) collective-permute-start(bf16[1,288,1152]{2,1,0:T(8,128)(2,1)S(1)} %slice.35), channel_id=1, source_target_pairs={{0,6},{1,3},{2,0},{3,5},{4,2},{5,7},{6,4},{7,1},{8,14},{9,11},{10,... | collective-permute-start | bytes 1990664 | tf_op jit(solution)/shard_map/ppermute | solution.py:392
  424.7 69.2 %copy-start.11 = (bf16[1,288,1152]{2,1,0:T(8,128)(2,1)}, bf16[1,288,1152]{2,1,0:T(8,128)(2,1)S(1)}, u32[]{:S(2)}) copy-start(bf16[1,288,1152]{2,1,0:T(8,128)(2,1)S(1)} %collective-permute-done.21.refs_0_) | copy-start | bytes 1990660
  424.7 17.6 %collective-permute-start.29 = (bf16[1,576,1152]{2,1,0:T(8,128)(2,1)S(1)}, bf16[1,576,1152]{2,1,0:T(8,128)(2,1)S(1)}, u32[]{:S(2)}, u32[]{:S(2)}) collective-permute-start(bf16[1,576,1152]{2,1,0:T(8,128)(2,1)S(1)} %collective-permute-done.23.refs_1_), channel_id=1, source_target_pairs={{0,1},{1,0},{2,3},{3,2},{4,5},{5,4},{6,7},{7,6},{8,9},{9,8},{10,11... | collective-permute-start | bytes 3981320 | tf_op jit(solution)/shard_map/ppermute | solution.py:392
  428.2 65.7 %copy-start.12 = (bf16[1,288,1152]{2,1,0:T(8,128)(2,1)}, bf16[1,288,1152]{2,1,0:T(8,128)(2,1)S(1)}, u32[]{:S(2)}) copy-start(bf16[1,288,1152]{2,1,0:T(8,128)(2,1)S(1)} %collective-permute-done.24.refs_1_) | copy-start | bytes 1990660
  428.2 65.1 %collective-permute-start.6 = (bf16[2,144,4608]{2,1,0:T(8,128)(2,1)S(1)}, bf16[2,144,4608]{2,1,0:T(8,128)(2,1)}, u32[]{:S(2)}, u32[]{:S(2)}) collective-permute-start(bf16[2,144,4608]{2,1,0:T(8,128)(2,1)S(1)} %copy-done.6), channel_id=1, source_target_pairs={{0,2},{1,7},{2,4},{3,1},{4,6},{5,3},{6,0},{7,5},{8,10},{9,15},{10,... | collective-permute-start | bytes 7962632 | tf_op jit(solution)/shard_map/ppermute | solution.py:392
  438.9 54.4 %collective-permute-start.8 = (bf16[2,144,4608]{2,1,0:T(8,128)(2,1)S(1)}, bf16[2,144,4608]{2,1,0:T(8,128)(2,1)}, u32[]{:S(2)}, u32[]{:S(2)}) collective-permute-start(bf16[2,144,4608]{2,1,0:T(8,128)(2,1)S(1)} %copy-done.6), channel_id=1, source_target_pairs={{0,6},{1,3},{2,0},{3,5},{4,2},{5,7},{6,4},{7,1},{8,14},{9,11},{10,... | collective-permute-start | bytes 7962632 | tf_op jit(solution)/shard_map/ppermute | solution.py:392
  441.7 3.1 collective-permute-start.26
  441.7 51.6 %copy-start.7 = (bf16[1,576,1152]{2,1,0:T(8,128)(2,1)}, bf16[1,576,1152]{2,1,0:T(8,128)(2,1)S(1)}, u32[]{:S(2)}) copy-start(bf16[1,576,1152]{2,1,0:T(8,128)(2,1)S(1)} %collective-permute-done.28.refs_2_) | copy-start | bytes 3981316
  441.7 4.9 collective-permute-start.27
  442.3 51.6 %copy-start.8 = (bf16[1,576,1152]{2,1,0:T(8,128)(2,1)}, bf16[1,576,1152]{2,1,0:T(8,128)(2,1)S(1)}, u32[]{:S(2)}) copy-start(bf16[1,576,1152]{2,1,0:T(8,128)(2,1)S(1)} %collective-permute-done.29.refs_3_) | copy-start | bytes 3981316
  442.3 5.3 collective-permute-start.22
  444.8 49.1 %copy-start.9 = (bf16[1,576,1152]{2,1,0:T(8,128)(2,1)}, bf16[1,576,1152]{2,1,0:T(8,128)(2,1)S(1)}, u32[]{:S(2)}) copy-start(bf16[1,576,1152]{2,1,0:T(8,128)(2,1)S(1)} %collective-permute-done.26.refs_0_) | copy-start | bytes 3981316
  444.8 71.0 %collective-permute-start.4 = (bf16[2,144,4608]{2,1,0:T(8,128)(2,1)}, bf16[2,144,4608]{2,1,0:T(8,128)(2,1)}, u32[]{:S(2)}, u32[]{:S(2)}) collective-permute-start(bf16[2,144,4608]{2,1,0:T(8,128)(2,1)} %get-tuple-element.27.refs_1_), channel_id=1, source_target_pairs={{0,1},{1,0},{2,3},{3,2},{4,5},{5,4},{6,7},{7,6},{8,9},{9,8},{10,11... | collective-permute-start | bytes 7962632 | tf_op jit(solution)/shard_map/ppermute | solution.py:392
  446.7 47.2 %copy-start.10 = (bf16[1,576,1152]{2,1,0:T(8,128)(2,1)}, bf16[1,576,1152]{2,1,0:T(8,128)(2,1)S(1)}, u32[]{:S(2)}) copy-start(bf16[1,576,1152]{2,1,0:T(8,128)(2,1)S(1)} %collective-permute-done.27.refs_1_) | copy-start | bytes 3981316
  446.7 69.1 %collective-permute-start.5 = (bf16[2,144,4608]{2,1,0:T(8,128)(2,1)}, bf16[2,144,4608]{2,1,0:T(8,128)(2,1)}, u32[]{:S(2)}, u32[]{:S(2)}) collective-permute-start(bf16[2,144,4608]{2,1,0:T(8,128)(2,1)} %get-tuple-element.29.refs_2_), channel_id=1, source_target_pairs={{0,1},{1,0},{2,3},{3,2},{4,5},{5,4},{6,7},{7,6},{8,9},{9,8},{10,11... | collective-permute-start | bytes 7962632 | tf_op jit(solution)/shard_map/ppermute | solution.py:392
  447.6 46.3 %copy-start.13 = (bf16[1,288,1152]{2,1,0:T(8,128)(2,1)}, bf16[1,288,1152]{2,1,0:T(8,128)(2,1)S(1)}, u32[]{:S(2)}) copy-start(bf16[1,288,1152]{2,1,0:T(8,128)(2,1)S(1)} %collective-permute-done.22.refs_0_) | copy-start | bytes 1990660
  447.6 8.5 %collective-permute-start.25 = (bf16[1,288,1152]{2,1,0:T(8,128)(2,1)S(1)}, bf16[1,288,1152]{2,1,0:T(8,128)(2,1)S(1)}, u32[]{:S(2)}, u32[]{:S(2)}) collective-permute-start(bf16[1,288,1152]{2,1,0:T(8,128)(2,1)S(1)} %collective-permute-done.24.refs_1_), channel_id=1, source_target_pairs={{0,1},{1,0},{2,3},{3,2},{4,5},{5,4},{6,7},{7,6},{8,9},{9,8},{10,11... | collective-permute-start | bytes 1990664 | tf_op jit(solution)/shard_map/ppermute | solution.py:392
  456.1 37.7 %copy-start.14 = (bf16[1,288,1152]{2,1,0:T(8,128)(2,1)}, bf16[1,288,1152]{2,1,0:T(8,128)(2,1)S(1)}, u32[]{:S(2)}) copy-start(bf16[1,288,1152]{2,1,0:T(8,128)(2,1)S(1)} %collective-permute-done.25.refs_1_) | copy-start | bytes 1990660
  456.1 60.7 %collective-permute-start.2 = (bf16[1,144,4608]{2,1,0:T(8,128)(2,1)}, bf16[1,144,4608]{2,1,0:T(8,128)(2,1)}, u32[]{:S(2)}, u32[]{:S(2)}) collective-permute-start(bf16[1,144,4608]{2,1,0:T(8,128)(2,1)} %collective-permute-done.refs_0_), channel_id=1, source_target_pairs={{0,1},{1,0},{2,3},{3,2},{4,5},{5,4},{6,7},{7,6},{8,9},{9,8},{10,11... | collective-permute-start | bytes 3981320 | tf_op jit(solution)/shard_map/ppermute | solution.py:392
  493.3 19.8 %collective-permute-start.16 = (bf16[1,288,1152]{2,1,0:T(8,128)(2,1)}, bf16[1,288,1152]{2,1,0:T(8,128)(2,1)}, u32[]{:S(2)}, u32[]{:S(2)}) collective-permute-start(bf16[1,288,1152]{2,1,0:T(8,128)(2,1)} %collective-permute-done.15.refs_0_), channel_id=1, source_target_pairs={{0,1},{1,0},{2,3},{3,2},{4,5},{5,4},{6,7},{7,6},{8,9},{9,8},{10,11... | collective-permute-start | bytes 1990664 | tf_op jit(solution)/shard_map/ppermute | solution.py:392
  493.3 19.8 %collective-permute-start.19 = (bf16[1,288,1152]{2,1,0:T(8,128)(2,1)}, bf16[1,288,1152]{2,1,0:T(8,128)(2,1)}, u32[]{:S(2)}, u32[]{:S(2)}) collective-permute-start(bf16[1,288,1152]{2,1,0:T(8,128)(2,1)} %collective-permute-done.18.refs_1_), channel_id=1, source_target_pairs={{0,1},{1,0},{2,3},{3,2},{4,5},{5,4},{6,7},{7,6},{8,9},{9,8},{10,11... | collective-permute-start | bytes 1990664 | tf_op jit(solution)/shard_map/ppermute | solution.py:392
  508.0 8.9 %copy-start.4 = (bf16[2,144,4608]{2,1,0:T(8,128)(2,1)S(1)}, bf16[2,144,4608]{2,1,0:T(8,128)(2,1)}, u32[]{:S(2)}) copy-start(bf16[2,144,4608]{2,1,0:T(8,128)(2,1)} %get-tuple-element.41) | copy-start | bytes 7962628
  513.1 44.8 %collective-permute-start.3 = (bf16[1,144,4608]{2,1,0:T(8,128)(2,1)}, bf16[1,144,4608]{2,1,0:T(8,128)(2,1)}, u32[]{:S(2)}, u32[]{:S(2)}) collective-permute-start(bf16[1,144,4608]{2,1,0:T(8,128)(2,1)} %collective-permute-done.1.refs_1_), channel_id=1, source_target_pairs={{0,1},{1,0},{2,3},{3,2},{4,5},{5,4},{6,7},{7,6},{8,9},{9,8},{10,11... | collective-permute-start | bytes 3981320 | tf_op jit(solution)/shard_map/ppermute | solution.py:392
  513.2 49.0 %collective-permute-start.7 = (bf16[1,144,4608]{2,1,0:T(8,128)(2,1)}, bf16[1,144,4608]{2,1,0:T(8,128)(2,1)}, u32[]{:S(2)}, u32[]{:S(2)}) collective-permute-start(bf16[1,144,4608]{2,1,0:T(8,128)(2,1)} %slice.32), channel_id=1, source_target_pairs={{0,2},{1,7},{2,4},{3,1},{4,6},{5,3},{6,0},{7,5},{8,10},{9,15},{10,... | collective-permute-start | bytes 3981320 | tf_op jit(solution)/shard_map/ppermute | solution.py:392
  515.8 46.9 %collective-permute-start.9 = (bf16[1,144,4608]{2,1,0:T(8,128)(2,1)}, bf16[1,144,4608]{2,1,0:T(8,128)(2,1)}, u32[]{:S(2)}, u32[]{:S(2)}) collective-permute-start(bf16[1,144,4608]{2,1,0:T(8,128)(2,1)} %slice.33), channel_id=1, source_target_pairs={{0,6},{1,3},{2,0},{3,5},{4,2},{5,7},{6,4},{7,1},{8,14},{9,11},{10,... | collective-permute-start | bytes 3981320 | tf_op jit(solution)/shard_map/ppermute | solution.py:392
  515.8 57.5 %collective-permute-start.12 = (bf16[2,144,4608]{2,1,0:T(8,128)(2,1)}, bf16[2,144,4608]{2,1,0:T(8,128)(2,1)}, u32[]{:S(2)}, u32[]{:S(2)}) collective-permute-start(bf16[2,144,4608]{2,1,0:T(8,128)(2,1)} %collective-permute-done.6.refs_1_), channel_id=1, source_target_pairs={{0,1},{1,0},{2,3},{3,2},{4,5},{5,4},{6,7},{7,6},{8,9},{9,8},{10,11... | collective-permute-start | bytes 7962632 | tf_op jit(solution)/shard_map/ppermute | solution.py:392
  516.9 56.4 %collective-permute-start.13 = (bf16[2,144,4608]{2,1,0:T(8,128)(2,1)}, bf16[2,144,4608]{2,1,0:T(8,128)(2,1)}, u32[]{:S(2)}, u32[]{:S(2)}) collective-permute-start(bf16[2,144,4608]{2,1,0:T(8,128)(2,1)} %collective-permute-done.8.refs_2_), channel_id=1, source_target_pairs={{0,1},{1,0},{2,3},{3,2},{4,5},{5,4},{6,7},{7,6},{8,9},{9,8},{10,11... | collective-permute-start | bytes 7962632 | tf_op jit(solution)/shard_map/ppermute | solution.py:392
  562.2 23.1 %collective-permute-start.10 = (bf16[1,144,4608]{2,1,0:T(8,128)(2,1)}, bf16[1,144,4608]{2,1,0:T(8,128)(2,1)}, u32[]{:S(2)}, u32[]{:S(2)}) collective-permute-start(bf16[1,144,4608]{2,1,0:T(8,128)(2,1)} %collective-permute-done.7.refs_0_), channel_id=1, source_target_pairs={{0,1},{1,0},{2,3},{3,2},{4,5},{5,4},{6,7},{7,6},{8,9},{9,8},{10,11... | collective-permute-start | bytes 3981320 | tf_op jit(solution)/shard_map/ppermute | solution.py:392
  562.7 22.6 %collective-permute-start.11 = (bf16[1,144,4608]{2,1,0:T(8,128)(2,1)}, bf16[1,144,4608]{2,1,0:T(8,128)(2,1)}, u32[]{:S(2)}, u32[]{:S(2)}) collective-permute-start(bf16[1,144,4608]{2,1,0:T(8,128)(2,1)} %collective-permute-done.9.refs_1_), channel_id=1, source_target_pairs={{0,1},{1,0},{2,3},{3,2},{4,5},{5,4},{6,7},{7,6},{8,9},{9,8},{10,11... | collective-permute-start | bytes 3981320 | tf_op jit(solution)/shard_map/ppermute | solution.py:392
